TPU v7x, 128 devices: a whole 4x4x4 slice. The times are simulated.
128 devices in a mesh: rows: 16 (over z_lo, y, core), width: 8 (over z_hi, x).
Axes of the slice: x: 4, y: 4, z: 4 (z_hi: 2, z_lo: 2; z = z_hi * 2 + z_lo), core: 2. Of those that a mesh axis runs over, the one named last changes fastest.
Arguments:
- one_query: float32 [7168, 7168], P('rows', 'width'), may hold values from -0.09375 to 0.09375
- other_query: float32 [7168, 7168], P('rows', 'width'), may hold values from -0.0625 to 0.0625
- one_key: float32 [7168, 1024], P('rows', 'width'), may hold values from -0.09375 to 0.09375
- other_key: float32 [7168, 1024], P('rows', 'width'), may hold values from -0.0625 to 0.0625
- one_value: float32 [7168, 1024], P('rows', 'width'), may hold values from -0.09375 to 0.09375
- other_value: float32 [7168, 1024], P('rows', 'width'), may hold values from -0.0625 to 0.0625
- mix_share: float32 [7168], P('rows'), may hold values from 0.2 to 0.8
- norm_train: float32 [7168], P(('rows', 'width')), may hold values from 0.25 to 1.75
- norm_step: float32 [7168], P(('rows', 'width')), may hold values from -0.3 to 0.3
Outputs:
- final_query: bfloat16 [7168, 7168], P(None, 'width')
- final_key: bfloat16 [7168, 1024], P(None, 'width')
- final_value: bfloat16 [7168, 1024], P(None, 'width')
- column_query: float32 [7168], P('width')
- column_key: float32 [1024], P('width')
- column_value: float32 [1024], P('width')
- serve_norm: bfloat16 [7168], replicated
All inputs are finite; a program needn't handle non-finite values.
Results may differ from a plain program's by a relative error of at most 0.001.
Values may be sent and summed in bfloat16 or wider, within the bound.
A program may use at most 128 MiB of HBM per device.

v0:
```python
import jax
import jax.numpy as jnp
from jax import lax
from jax.sharding import PartitionSpec as P


def from_everyone(x, axis):
    copies = jnp.broadcast_to(x, (lax.axis_size(axis), *x.shape))
    return lax.all_to_all(copies, axis, split_axis=0, concat_axis=0, tiled=True)


def of_everyone(x, axis):
    everything = from_everyone(x, axis)
    return jnp.sum(everything, axis=0)


def packed_total(arrays, axis):
    flat, at, finished = (jnp.concatenate([a.reshape(-1) for a in arrays]), 0, [])
    subtotal = of_everyone(flat, axis)
    for a in arrays:
        finished.append(subtotal[at : at + a.size].reshape(a.shape))
        at += a.size
    return tuple(finished)


def side_by_side(arrays, axis, dim, along):
    both = jnp.concatenate(arrays, axis=along)
    result, at, finished = (lax.all_gather(both, axis, axis=dim, tiled=True), 0, [])
    for a in arrays:
        finished.append(lax.slice_in_dim(result, at, at + a.shape[along], axis=along))
        at += a.shape[along]
    return tuple(finished)


def shards(
    one_query,
    other_query,
    one_key,
    other_key,
    one_value,
    other_value,
    mix_share,
    norm_train,
    norm_step,
):
    result_query = mix_share[:, None] * one_query + (1.0 - mix_share[:, None]) * other_query
    result_key = mix_share[:, None] * one_key + (1.0 - mix_share[:, None]) * other_key
    result_value = mix_share[:, None] * one_value + (1.0 - mix_share[:, None]) * other_value
    total_query, total_key, total_value = packed_total(
        (
            jnp.sum(result_query * result_query, axis=0),
            jnp.sum(result_key * result_key, axis=0),
            jnp.sum(result_value * result_value, axis=0),
        ),
        "rows",
    )
    column_query = jnp.sqrt(total_query)
    column_key = jnp.sqrt(total_key)
    column_value = jnp.sqrt(total_value)
    narrow_query, narrow_key, narrow_value = (
        (result_query / column_query).astype(jnp.bfloat16),
        (result_key / column_key).astype(jnp.bfloat16),
        (result_value / column_value).astype(jnp.bfloat16),
    )
    final_query, final_key, final_value = side_by_side(
        (narrow_query, narrow_key, narrow_value), "rows", 0, 1
    )
    serve_norm = lax.all_gather(
        (norm_train + norm_step).astype(jnp.bfloat16), ("rows", "width"), axis=0, tiled=True
    )
    return (final_query, final_key, final_value, column_query, column_key, column_value, serve_norm)


def solution(mesh):
    in_specs = (
        P("rows", "width"),
        P("rows", "width"),
        P("rows", "width"),
        P("rows", "width"),
        P("rows", "width"),
        P("rows", "width"),
        P("rows"),
        P(("rows", "width")),
        P(("rows", "width")),
    )
    out_specs = (
        P(None, "width"),
        P(None, "width"),
        P(None, "width"),
        P("width"),
        P("width"),
        P("width"),
        P(),
    )
    return jax.shard_map(shards, mesh=mesh, in_specs=in_specs, out_specs=out_specs, check_vma=False)
```

profile of v0, /device:TPU:1, one launch (start us, length us, event | category | flops | bytes accessed | tf_op | source)
XLA Modules:
  0.0 141.1 jit_solution(13820598020973978028)
XLA Ops:
  7.2 0.0 all-gather.2.cloned.1.call-start
  7.2 0.7 broadcast_subtract_fusion
  7.9 2.4 %multiply_reduce_fusion = f32[896]{0:T(1024)S(1)} fusion(f32[448,896]{1,0:T(8,128)} %param.10, f32[448]{0:T(512)S(1)} %broadcast_subtract_fusion, f32[448,896]{1,0:T(8,128)} %param.9, f32[448]{0:T(512)} %param.15), kind=kLoop, calls=%fused_computation.1 | loop fusion | flops 2006144 | bytes 3218432 | tf_op jit(solution)/shard_map/reduce_sum | solution.py:51
  10.3 1.5 %multiply_reduce_fusion.2 = (f32[128]{0:T(128)S(1)}, f32[128]{0:T(128)S(1)}) fusion(f32[448,128]{1,0:T(8,128)} %param.12, f32[448]{0:T(512)S(1)} %broadcast_subtract_fusion, f32[448,128]{1,0:T(8,128)} %param.11, f32[448]{0:T(512)S(1)} %copy-done.6, f32[448,128]{1,0:T(8,128)} %param.14, f32[448,128]{1,0:T(8,128)} %param.13), kind=kLoop, calls=%fused_computation.8 | loop fusion | flops 573184 | bytes 922112 | tf_op jit(solution)/shard_map/reduce_sum | solution.py:52
  11.9 13.0 %all_to_all.6 = f32[16,1,1152]{2,1,0:T(1,128)S(1)} all-to-all(f32[16,1,1152]{2,1,0:T(1,128)S(1)} %broadcast_in_dim.2), channel_id=1, replica_groups=mesh['rows'=16,'width'=8] {'rows'}, dimensions={0} | all-to-all | bytes 147456 | tf_op jit(solution)/shard_map/all_to_all | solution.py:9
  24.8 0.1 reduce_sum.39
  24.9 0.0 copy-start.8
  24.9 0.0 copy-start.9
  24.9 0.0 copy-start.7
  25.0 0.0 copy-start.3
  25.0 0.3 divide_convert_fusion
  25.3 0.2 copy-done.7
  25.5 0.4 copy-done.2
  25.9 0.1 copy-done.3
  26.0 0.1 copy-done.4
  26.1 0.1 copy-done.5
  26.2 0.2 divide_convert_fusion.2
  26.5 1.1 pad_maximum_fusion
  27.5 0.0 all-gather.2.cloned.1.call-update
  27.6 0.2 dynamic-update-slice
  27.8 65.5 %all-reduce = bf16[7168]{0:T(1024)(128)(2,1)} all-reduce(bf16[7168]{0:T(1024)(128)(2,1)S(1)} %dynamic-update-slice), channel_id=1, replica_groups=mesh['rows'=16,'width'=8] {'rows','width'}, use_global_device_ids=true, to_apply=%add | all-reduce | flops 7168 | bytes 28672
  93.3 26.1 %all-gather.2.cloned.1.call-done = bf16[7168,1152]{1,0:T(8,128)(2,1)} async-done(((bf16[448,1152]{1,0:T(8,128)(2,1)}), bf16[7168,1152]{1,0:T(8,128)(2,1)}) %all-gather.2.cloned.1.call-update) | async-done | bytes 16515088 | tf_op jit(solution)/shard_map/all_gather | solution.py:28
  119.4 10.7 %slice.27 = bf16[7168,896]{1,0:T(8,128)(2,1)} slice(bf16[7168,1152]{1,0:T(8,128)(2,1)} %all-gather.2.cloned.1.call-done), slice={[0:7168], [0:896]} | slice | bytes 25690112 | tf_op jit(solution)/shard_map/slice | solution.py:30
  130.1 4.1 %fusion = (bf16[7168,128]{1,0:T(8,128)(2,1)}, bf16[7168,128]{1,0:T(8,128)(2,1)}) fusion(bf16[7168,1152]{1,0:T(8,128)(2,1)} %all-gather.2.cloned.1.call-done), kind=kLoop, calls=%fused_computation.16 | loop fusion | bytes 7340032 | tf_op jit(solution)/shard_map/slice | solution.py:30
  (21 shorter events, 0.1 us)
Async XLA Ops:
  7.2 112.3 %all-gather.2.cloned.1.call-start = ((), (), s32[]{:S(2)}) async-start(), calls=%async_computation.1 | async-start | bytes 17547264 | tf_op jit(solution)/shard_map/all_gather | solution.py:28
  7.9 2.4 %copy-start.6 = (f32[448]{0:T(512)S(1)}, f32[448]{0:T(512)}, u32[]{:S(2)}) copy-start(f32[448]{0:T(512)} %param.15) | copy-start | bytes 5380
  7.9 17.0 %copy-start = (f32[448,896]{1,0:T(8,128)S(1)}, f32[448,896]{1,0:T(8,128)}, u32[]{:S(2)}) copy-start(f32[448,896]{1,0:T(8,128)} %param.10) | copy-start | bytes 4816900
  7.9 17.0 %copy-start.1 = (f32[448,896]{1,0:T(8,128)S(1)}, f32[448,896]{1,0:T(8,128)}, u32[]{:S(2)}) copy-start(f32[448,896]{1,0:T(8,128)} %param.9) | copy-start | bytes 4816900
  24.9 0.7 copy-start.8
  24.9 0.6 copy-start.9
  24.9 0.6 copy-start.7
  25.0 0.9 copy-start.2
  25.0 1.0 copy-start.3
  25.0 1.1 copy-start.4
  25.0 1.3 copy-start.5
  26.4 1.1 copy-start.10
  26.4 1.1 copy-start.11
Sparse Core Ops, SparseCore 0:
  27.7 91.7 all-gather.1
where the time goes:
time: 141 us
  blocking collectives  78.5 us (56%)
  waiting for transfers between devices  26.1 us (19%)
  local copies, waits for them, and re-layouts  16.1 us (11%)
  between operations  14.2 us (10%)
  other arithmetic  6.18 us (4%)
    unnamed x1, blocking collectives  65.5 us
    all_gather x1, waiting for transfers between devices, side_by_side(): lax.all_gather(both, axis, axis=dim, tiled=True)  26.1 us
    slice x2, local copies, waits for them, and re-layouts, side_by_side(): lax.slice_in_dim(result, at, at + a.shape[along], axis=along)  14.8 us
    all_to_all x1, blocking collectives, from_everyone(): return lax.all_to_all(copies, axis, split_axis=0, concat_axis=0, tiled=True)  13 us
  transfers between devices with their start and end apart: 1, of which 1 were waited for; matrix products, arithmetic and copies ran while one was open for 0% of the time, Pallas kernels for 0%

commit v1 on v0

v1 whole, which is shorter than its diff:
```python
import jax
import jax.numpy as jnp
from jax import lax
from jax.experimental import pallas as pl
from jax.experimental.pallas import tpu as pltpu
from jax.sharding import PartitionSpec as P

MESH = pl.DeviceIdType.MESH
LANES = 128
DEVICES = 16
PEERS = 8
NORM = 56

PIECES = ((0, 96), (96, 96), (192, 128), (320, 128))
LOADS = 4


def gather_kernel(
    one_query,
    other_query,
    one_key,
    other_key,
    one_value,
    other_value,
    mix,
    train,
    step,
    blocks,
    scale_query,
    scale_key,
    scale_value,
    serve,
    ones,
    others,
    mixed,
    shares,
    share_row,
    mix_here,
    train_here,
    step_here,
    sums,
    norm_row,
    norm_images,
    norm_pairs,
    norm_all,
    load_sem,
    small_sem,
    send_sem,
    recv_sem,
    sum_send,
    sum_recv,
    image_send,
    image_recv,
    pair_send,
    pair_recv,
):
    depth = mixed.shape[0]
    me = lax.axis_index("rows")
    place = lax.axis_index("width")
    core = lax.rem(me, 2)
    y = lax.rem(lax.div(me, 2), 4)
    z = lax.div(me, 8)

    def device(dz, dy, other=0):
        return lax.rem(z + dz, 2) * 8 + lax.rem(y + dy, 4) * 2 + lax.rem(core + other, 2)

    up, down, across, sibling = device(0, 1), device(0, 3), device(1, 0), device(0, 0, 1)

    small = []
    for i, (source, target) in enumerate(
        ((mix, mix_here), (train, train_here), (step, step_here))
    ):
        copy = pltpu.make_async_copy(source, target, small_sem.at[i])
        copy.start()
        small.append(copy)
    pairs = ((one_query, other_query), (one_key, other_key), (one_value, other_value))
    chunk = depth // LOADS
    loads = []
    for i in range(LOADS):
        mine = []
        at = 0
        for a, (one, other) in enumerate(pairs):
            wide = one.shape[1]
            for b, (source, target) in enumerate(((one, ones), (other, others))):
                rows = pl.ds(i * chunk, chunk)
                copy = pltpu.make_async_copy(
                    source.at[rows, :], target.at[rows, pl.ds(at, wide)], load_sem.at[i, 2 * a + b]
                )
                copy.start()
                mine.append(copy)
            at += wide
        loads.append(mine)

    barrier = pltpu.get_barrier_semaphore()
    for j in range(1, DEVICES):
        pl.semaphore_signal(
            barrier, inc=1, device_id={"rows": lax.rem(me + j, DEVICES)}, device_id_type=MESH
        )
    for j in range(1, PEERS):
        pl.semaphore_signal(
            barrier, inc=1, device_id={"width": lax.rem(place + j, PEERS)}, device_id_type=MESH
        )

    for copy in small:
        copy.wait()

    share_row[...] = jnp.zeros_like(share_row)
    share_row[:, pl.ds(0, depth)] = mix_here[...]
    for i in range(shares.shape[0] // LANES):
        row = share_row[:, pl.ds(i * LANES, LANES)]
        shares[pl.ds(i * LANES, LANES), :] = jnp.broadcast_to(row, (LANES, LANES)).T

    norm_row[...] = jnp.zeros_like(norm_row)
    norm_row[:, pl.ds(0, NORM)] = train_here[...] + step_here[...]
    first = (lax.rem(me, 2) * PEERS + place) * NORM
    gains = jnp.broadcast_to(norm_row[...], (8, LANES))
    gains = pltpu.roll(gains, lax.rem(first, LANES), 1)
    flat = lax.broadcasted_iota(jnp.int32, (8, LANES), 0) * LANES + lax.broadcasted_iota(
        jnp.int32, (8, LANES), 1
    )
    inside = (flat >= first) & (flat < first + NORM)
    norm_images[place] = jnp.where(inside, gains, 0.0)

    tiles = mixed.shape[1] // LANES

    def mix_rows(strip, partial):
        rows = pl.ds(pl.multiple_of(strip * 8, 8), 8)
        share = shares[rows, :]
        rest = 1.0 - share
        found = []
        for t in range(tiles):
            lanes = pl.ds(t * LANES, LANES)
            value = share * ones[rows, lanes] + rest * others[rows, lanes]
            mixed[rows, lanes] = value
            found.append(partial[t] + value * value)
        return tuple(found)

    partial = tuple(jnp.zeros((8, LANES), jnp.float32) for _ in range(tiles))
    for i in range(LOADS):
        for copy in loads[i]:
            copy.wait()
        partial = lax.fori_loop(i * chunk // 8, (i + 1) * chunk // 8, mix_rows, partial, unroll=2)
    for t in range(tiles):
        sums[me, :, pl.ds(t * LANES, LANES)] = jnp.sum(partial[t], axis=0, keepdims=True)

    pl.semaphore_wait(barrier, DEVICES - 1 + PEERS - 1)

    sum_copies = []
    for j in range(1, DEVICES):
        copy = pltpu.make_async_remote_copy(
            src_ref=sums.at[me],
            dst_ref=sums.at[me],
            send_sem=sum_send.at[j],
            recv_sem=sum_recv.at[me],
            device_id={"rows": lax.rem(me + j, DEVICES)},
            device_id_type=MESH,
        )
        copy.start()
        sum_copies.append(copy)
    image_copies = []
    for j in range(1, PEERS):
        copy = pltpu.make_async_remote_copy(
            src_ref=norm_images.at[place],
            dst_ref=norm_images.at[place],
            send_sem=image_send.at[j],
            recv_sem=image_recv.at[place],
            device_id={"width": lax.rem(place + j, PEERS)},
            device_id_type=MESH,
        )
        copy.start()
        image_copies.append(copy)

    for j in range(1, DEVICES):
        source = lax.rem(me + j, DEVICES)
        pltpu.make_async_remote_copy(
            src_ref=sums.at[source],
            dst_ref=sums.at[source],
            send_sem=sum_send.at[j],
            recv_sem=sum_recv.at[source],
            device_id={"rows": source},
            device_id_type=MESH,
        ).wait_recv()

    total = sums[0]
    for j in range(1, DEVICES):
        total = total + sums[j]
    scale = jnp.sqrt(total)
    t = 0
    for out in (scale_query, scale_key, scale_value):
        for i in range(out.shape[0]):
            out[i : i + 1, :] = scale[:, t * LANES : (t + 1) * LANES]
            t += 1
    inverse = 1.0 / scale
    factors = [
        jnp.broadcast_to(inverse[:, t * LANES : (t + 1) * LANES], (16, LANES)) for t in range(tiles)
    ]

    def narrow(piece):
        start, count = PIECES[piece]

        def body(strip, carry):
            rows = pl.ds(pl.multiple_of(start + strip * 16, 16), 16)
            for t in range(tiles):
                lanes = pl.ds(t * LANES, LANES)
                blocks[me, rows, lanes] = (mixed[rows, lanes] * factors[t]).astype(jnp.bfloat16)
            return carry

        lax.fori_loop(0, count // 16, body, 0, unroll=2)

    sent = []

    def send(block, piece, target):
        rows = pl.ds(*PIECES[piece])
        copy = pltpu.make_async_remote_copy(
            src_ref=blocks.at[block, rows, :],
            dst_ref=blocks.at[block, rows, :],
            send_sem=send_sem.at[len(sent)],
            recv_sem=recv_sem.at[block, piece],
            device_id={"rows": target},
            device_id_type=MESH,
        )
        copy.start()
        sent.append(copy)

    def arrived(block, piece):
        rows = pl.ds(*PIECES[piece])
        pltpu.make_async_remote_copy(
            src_ref=blocks.at[block, rows, :],
            dst_ref=blocks.at[block, rows, :],
            send_sem=send_sem.at[0],
            recv_sem=recv_sem.at[block, piece],
            device_id={"rows": sibling},
            device_id_type=MESH,
        ).wait_recv()

    narrow(0)
    send(me, 0, up)
    narrow(1)
    send(me, 1, down)
    send(me, 1, up)
    send(me, 0, down)
    narrow(2)
    send(me, 2, across)
    send(me, 2, up)
    narrow(3)
    send(me, 3, down)
    send(me, 3, across)
    send(me, 3, up)
    send(me, 2, down)
    send(me, 0, across)
    send(me, 1, across)
    for piece in range(4):
        send(me, piece, sibling)

    for j in range(1, PEERS):
        source = lax.rem(place + j, PEERS)
        pltpu.make_async_remote_copy(
            src_ref=norm_images.at[source],
            dst_ref=norm_images.at[source],
            send_sem=image_send.at[j],
            recv_sem=image_recv.at[source],
            device_id={"width": source},
            device_id_type=MESH,
        ).wait_recv()
    image = norm_images[0]
    for j in range(1, PEERS):
        image = image + norm_images[j]
    norm_pairs[me] = image
    pair_copies = []
    for j in range(1, DEVICES):
        copy = pltpu.make_async_remote_copy(
            src_ref=norm_pairs.at[me],
            dst_ref=norm_pairs.at[me],
            send_sem=pair_send.at[j],
            recv_sem=pair_recv.at[me],
            device_id={"rows": lax.rem(me + j, DEVICES)},
            device_id_type=MESH,
        )
        copy.start()
        pair_copies.append(copy)

    below, above, far = device(0, 3), device(0, 1), device(0, 2)
    side, side_below, side_above, side_far = device(1, 0), device(1, 3), device(1, 1), device(1, 2)
    seen = set()
    for block, piece, targets in (
        (below, 0, (up, across)),
        (above, 1, (down, across)),
        (side, 2, (up,)),
        (below, 1, (across,)),
        (above, 0, (across,)),
        (side, 3, (down, up)),
        (side, 2, (down,)),
        (below, 2, (up,)),
        (above, 3, (down,)),
        (side, 0, ()),
        (below, 3, ()),
        (above, 2, ()),
        (side, 1, ()),
        (far, 0, (across,)),
        (far, 1, (across,)),
        (side_below, 0, ()),
        (side_above, 1, ()),
        (side_below, 2, (up,)),
        (side_above, 3, (down,)),
        (side_below, 1, ()),
        (side_below, 3, ()),
        (side_above, 2, ()),
        (side_above, 0, ()),
        (far, 2, ()),
        (far, 3, ()),
        (side_far, 0, ()),
        (side_far, 1, ()),
        (side_far, 2, ()),
        (side_far, 3, ()),
    ):
        if (id(block), piece) not in seen:
            seen.add((id(block), piece))
            arrived(block, piece)
            send(block, piece, sibling)
        for target in targets:
            send(block, piece, target)

    for j in range(1, DEVICES):
        source = lax.rem(me + j, DEVICES)
        pltpu.make_async_remote_copy(
            src_ref=norm_pairs.at[source],
            dst_ref=norm_pairs.at[source],
            send_sem=pair_send.at[j],
            recv_sem=pair_recv.at[source],
            device_id={"rows": source},
            device_id_type=MESH,
        ).wait_recv()
    for j in range(DEVICES // 2):
        both = norm_pairs[2 * j] + norm_pairs[2 * j + 1]
        norm_all[pl.ds(7 * j, 8), :] = both
    serve[...] = norm_all[pl.ds(0, NORM), :].astype(serve.dtype)

    for dz in range(2):
        for dy in range(4):
            for piece in range(4):
                arrived(device(dz, dy, 1), piece)
    for copy in sent + sum_copies + image_copies + pair_copies:
        copy.wait_send()


def write_kernel(
    blocks,
    scale_query,
    scale_key,
    scale_value,
    serve,
    query,
    key,
    value,
    query_scale,
    key_scale,
    value_scale,
    gains,
    sem,
    small_sem,
):
    depth = blocks.shape[1]
    copies = []
    for b in range(DEVICES):
        at = 0
        for n, out in enumerate((query, key, value)):
            wide = out.shape[1]
            copy = pltpu.make_async_copy(
                blocks.at[b, :, pl.ds(at, wide)], out.at[pl.ds(b * depth, depth), :], sem.at[b, n]
            )
            copy.start()
            copies.append(copy)
            at += wide
    for i, (source, target) in enumerate(
        (
            (scale_query, query_scale),
            (scale_key, key_scale),
            (scale_value, value_scale),
            (serve, gains),
        )
    ):
        copy = pltpu.make_async_copy(source, target, small_sem.at[i])
        copy.start()
        copies.append(copy)
    for copy in copies:
        copy.wait()


def shards(
    one_query,
    other_query,
    one_key,
    other_key,
    one_value,
    other_value,
    mix_share,
    norm_train,
    norm_step,
):
    f32, bf16 = jnp.float32, jnp.bfloat16
    depth, queries = one_query.shape
    keys = one_key.shape[1]
    wide = queries + 2 * keys
    tall = -(-depth // LANES) * LANES
    dma = pltpu.SemaphoreType.DMA
    hbm, vmem = pl.BlockSpec(memory_space=pltpu.HBM), pl.BlockSpec(memory_space=pltpu.VMEM)
    blocks, scale_query, scale_key, scale_value, serve = pl.pallas_call(
        gather_kernel,
        out_shape=(
            pltpu.VMEM((DEVICES, depth, wide), bf16),
            pltpu.VMEM((queries // LANES, LANES), f32),
            pltpu.VMEM((keys // LANES, LANES), f32),
            pltpu.VMEM((keys // LANES, LANES), f32),
            pltpu.VMEM((NORM, LANES), bf16),
        ),
        in_specs=[hbm] * 9,
        out_specs=[vmem] * 5,
        scratch_shapes=[
            pltpu.VMEM((depth, wide), f32),
            pltpu.VMEM((depth, wide), f32),
            pltpu.VMEM((depth, wide), f32),
            pltpu.VMEM((tall, LANES), f32),
            pltpu.VMEM((1, tall), f32),
            pltpu.VMEM((1, depth), f32),
            pltpu.VMEM((1, NORM), f32),
            pltpu.VMEM((1, NORM), f32),
            pltpu.VMEM((DEVICES, 1, wide), f32),
            pltpu.VMEM((1, LANES), f32),
            pltpu.VMEM((PEERS, 8, LANES), f32),
            pltpu.VMEM((DEVICES, 8, LANES), f32),
            pltpu.VMEM((64, LANES), f32),
            dma((LOADS, 6)),
            dma((3,)),
            dma((72,)),
            dma((DEVICES, 4)),
            dma((DEVICES,)),
            dma((DEVICES,)),
            dma((PEERS,)),
            dma((PEERS,)),
            dma((DEVICES,)),
            dma((DEVICES,)),
        ],
        compiler_params=pltpu.CompilerParams(
            collective_id=0, has_side_effects=True, vmem_limit_bytes=48 * 1024 * 1024
        ),
        name="gather",
    )(
        one_query,
        other_query,
        one_key,
        other_key,
        one_value,
        other_value,
        mix_share.reshape(1, depth),
        norm_train.reshape(1, NORM),
        norm_step.reshape(1, NORM),
    )
    finals = pl.pallas_call(
        write_kernel,
        out_shape=(
            jax.ShapeDtypeStruct((DEVICES * depth, queries), bf16),
            jax.ShapeDtypeStruct((DEVICES * depth, keys), bf16),
            jax.ShapeDtypeStruct((DEVICES * depth, keys), bf16),
            jax.ShapeDtypeStruct((queries // LANES, LANES), f32),
            jax.ShapeDtypeStruct((keys // LANES, LANES), f32),
            jax.ShapeDtypeStruct((keys // LANES, LANES), f32),
            jax.ShapeDtypeStruct((NORM, LANES), bf16),
        ),
        in_specs=[vmem] * 5,
        out_specs=[hbm] * 7,
        scratch_shapes=[dma((DEVICES, 3)), dma((4,))],
        compiler_params=pltpu.CompilerParams(vmem_limit_bytes=1024 * 1024),
        name="write",
    )(blocks, scale_query, scale_key, scale_value, serve)
    return finals[:3] + tuple(a.reshape(-1) for a in finals[3:])


def solution(mesh):
    in_specs = (
        P("rows", "width"),
        P("rows", "width"),
        P("rows", "width"),
        P("rows", "width"),
        P("rows", "width"),
        P("rows", "width"),
        P("rows"),
        P(("rows", "width")),
        P(("rows", "width")),
    )
    out_specs = (
        P(None, "width"),
        P(None, "width"),
        P(None, "width"),
        P("width"),
        P("width"),
        P("width"),
        P(),
    )
    return jax.shard_map(shards, mesh=mesh, in_specs=in_specs, out_specs=out_specs, check_vma=False)
```

time: 141 us -> 79.4 us (0.56)
  Pallas kernels: 0 us -> 78.6 us
  blocking collectives: 78.5 us -> 0 us
  waiting for transfers between devices: 26.1 us -> 0 us
  local copies, waits for them, and re-layouts: 16.1 us -> 0 us
  between operations: 14.2 us -> 0.64 us
  other arithmetic: 6.18 us -> 0 us
    pallas_call x0 -> x2, Pallas kernels: none -> 78.6 us  [the longest x1 72.4 us: shards(): pl.pallas_call(gather_kernel, out_shape=(pltpu.VMEM((DEVICES, depth, wide...]
    unnamed x1 -> x0, blocking collectives: 65.5 us -> none
    all_gather x1 -> x0, waiting for transfers between devices: 26.1 us -> none  [side_by_side(): lax.all_gather(both, axis, axis=dim, tiled=True)]
    slice x2 -> x0, local copies, waits for them, and re-layouts: 14.8 us -> none  [side_by_side(): lax.slice_in_dim(result, at, at + a.shape[along], axis=along)]
    all_to_all x1 -> x0, blocking collectives: 13 us -> none  [from_everyone(): return lax.all_to_all(copies, axis, split_axis=0, concat_axis=0, tiled=True)]
    reduce_sum x3 -> x0, other arithmetic: 3.92 us -> none  [the longest x1 2.39 us: shards(): jnp.sum(result_query * result_query, axis=0)]
  transfers between devices with their start and end apart: 1 -> 0, of which waited for: 1 -> 0; matrix products, arithmetic and copies ran while one was open for 0% -> 0% of each run, Pallas kernels for 0% -> 0%
where the time goes in v1:
time: 79.4 us; the launch traced here: 79.3 us
  Pallas kernels  78.6 us (99%)
    pallas_call x1, Pallas kernels, shards(): pl.pallas_call(gather_kernel, out_shape=(pltpu.VMEM((DEVICES, depth, wide...  72.4 us
    pallas_call x1, Pallas kernels, shards(): pl.pallas_call(write_kernel, out_shape=(jax.ShapeDtypeStruct((DEVICES * d...  6.19 us

profile of v1, /device:TPU:1, one launch (start us, length us, event | category | flops | bytes accessed | tf_op | source)
XLA Modules:
  0.0 79.3 jit_solution(12665976145226045832)
XLA Ops:
  0.6 72.4 %gather.1 = (bf16[16,448,1152]{2,1,0:T(8,128)(2,1)S(1)}, f32[7,128]{1,0:T(8,128)S(1)}, f32[1,128]{1,0:T(1,128)S(1)}, f32[1,128]{1,0:T(1,128)S(1)}, bf16[56,128]{1,0:T(8,128)(2,1)S(1)}) custom-call(f32[448,896]{1,0:T(8,128)} %one_query.1, f32[448,896]{1,0:T(8,128)} %other_query.1, f32[448,128]{1,0:T(8,128)} %one_key.1, f32[448,128]{1,0:T(8,128)} %other_key.1, ...), custom_call_target="tpu_custom_call" | custom-call | tf_op jit(solution)/shard_map/gather/pallas_call | solution.py:407
  73.1 6.2 %write.1 = (bf16[7168,896]{1,0:T(8,128)(2,1)}, bf16[7168,128]{1,0:T(8,128)(2,1)}, bf16[7168,128]{1,0:T(8,128)(2,1)}, f32[7,128]{1,0:T(8,128)}, f32[1,128]{1,0:T(...) custom-call(bf16[16,448,1152]{2,1,0:T(8,128)(2,1)S(1)} %get-tuple-element.19.blocks, ...), custom_call_target="tpu_custom_call" | custom-call | tf_op jit(solution)/shard_map/write/pallas_call | solution.py:458

commit v2 on v1

v2 whole, which is shorter than its diff:
```python
import jax
import jax.numpy as jnp
from jax import lax
from jax.experimental import pallas as pl
from jax.experimental.pallas import tpu as pltpu
from jax.sharding import PartitionSpec as P

MESH = pl.DeviceIdType.MESH
LANES = 128
DEVICES = 16
PEERS = 8
NORM = 56

PIECES = ((0, 96), (96, 96), (192, 128), (320, 128))
LOADS = 4


def gather_kernel(
    one_query,
    other_query,
    one_key,
    other_key,
    one_value,
    other_value,
    mix,
    train,
    step,
    blocks,
    scale_query,
    scale_key,
    scale_value,
    serve,
    both,
    mixed,
    shares,
    share_row,
    mix_here,
    train_here,
    step_here,
    sums,
    norm_row,
    norm_images,
    norm_pairs,
    norm_all,
    load_sem,
    small_sem,
    send_sem,
    recv_sem,
    sibling_sem,
    sum_sem,
    image_send,
    image_recv,
    pair_sem,
):
    depth, wide = mixed.shape
    tiles = wide // LANES
    me = lax.axis_index("rows")
    place = lax.axis_index("width")
    core = lax.rem(me, 2)
    y = lax.rem(lax.div(me, 2), 4)
    z = lax.div(me, 8)

    def device(dz, dy, other=0):
        return lax.rem(z + dz, 2) * 8 + lax.rem(y + dy, 4) * 2 + lax.rem(core + other, 2)

    def remote(ref, send, recv, **target):
        return pltpu.make_async_remote_copy(
            src_ref=ref,
            dst_ref=ref,
            send_sem=send,
            recv_sem=recv,
            device_id=target,
            device_id_type=MESH,
        )

    def wait_bytes(ref, sem):
        pltpu.make_async_copy(ref, ref, sem).wait()

    for i, (source, target) in enumerate(
        ((mix, mix_here), (train, train_here), (step, step_here))
    ):
        pltpu.make_async_copy(source, target, small_sem.at[i]).start()
    chunk = depth // LOADS
    for i in range(LOADS):
        rows = pl.ds(i * chunk, chunk)
        at = 0
        for pair in ((one_query, other_query), (one_key, other_key), (one_value, other_value)):
            for n, source in enumerate(pair):
                columns = pl.ds(at, source.shape[1])
                pltpu.make_async_copy(
                    source.at[rows, :], both.at[n, rows, columns], load_sem.at[i]
                ).start()
            at += pair[0].shape[1]

    barrier = pltpu.get_barrier_semaphore()
    for j in range(1, DEVICES):
        pl.semaphore_signal(
            barrier, inc=1, device_id={"rows": lax.rem(me + j, DEVICES)}, device_id_type=MESH
        )
    for j in range(1, PEERS):

        @pl.when(place + j < PEERS)
        def _():
            pl.semaphore_signal(
                barrier, inc=1, device_id={"width": place + j}, device_id_type=MESH
            )

    for i, target in enumerate((mix_here, train_here, step_here)):
        wait_bytes(target, small_sem.at[i])

    share_row[...] = jnp.zeros_like(share_row)
    share_row[:, pl.ds(0, depth)] = mix_here[...]
    for i in range(shares.shape[0] // LANES):
        row = share_row[:, pl.ds(i * LANES, LANES)]
        shares[pl.ds(i * LANES, LANES), :] = jnp.broadcast_to(row, (LANES, LANES)).T

    norm_row[...] = jnp.zeros_like(norm_row)
    norm_row[:, pl.ds(0, NORM)] = train_here[...] + step_here[...]
    first = (core * PEERS + place) * NORM
    gains = jnp.broadcast_to(norm_row[...], (8, LANES))
    gains = pltpu.roll(gains, lax.rem(first, LANES), 1)
    flat = lax.broadcasted_iota(jnp.int32, (8, LANES), 0) * LANES + lax.broadcasted_iota(
        jnp.int32, (8, LANES), 1
    )
    inside = (flat >= first) & (flat < first + NORM)
    norm_images[place] = jnp.where(inside, gains, 0.0)

    def mix_rows(strip, partial):
        rows = pl.ds(pl.multiple_of(strip * 8, 8), 8)
        share = shares[rows, :]
        rest = 1.0 - share
        found = []
        for t in range(tiles):
            lanes = pl.ds(t * LANES, LANES)
            value = share * both[0, rows, lanes] + rest * both[1, rows, lanes]
            mixed[rows, lanes] = value
            found.append(partial[t] + value * value)
        return tuple(found)

    partial = tuple(jnp.zeros((8, LANES), jnp.float32) for _ in range(tiles))
    for i in range(LOADS):
        wait_bytes(both.at[:, pl.ds(i * chunk, chunk), :], load_sem.at[i])
        partial = lax.fori_loop(i * chunk // 8, (i + 1) * chunk // 8, mix_rows, partial, unroll=2)
    for t in range(tiles):
        sums[me, :, pl.ds(t * LANES, LANES)] = jnp.sum(partial[t], axis=0, keepdims=True)

    pl.semaphore_wait(barrier, DEVICES - 1 + place)

    for j in range(1, DEVICES):
        remote(sums.at[me], sum_sem.at[0], sum_sem.at[1], rows=lax.rem(me + j, DEVICES)).start()

    def image_copy(source, target):
        return remote(norm_images.at[source], image_send.at[0], image_recv.at[source], width=target)

    for j in range(1, PEERS):

        @pl.when(place + j >= PEERS)
        def _():
            image_copy(place, place + j - PEERS).start()

    wait_bytes(sums.at[pl.ds(0, DEVICES - 1)], sum_sem.at[1])
    total = sums[0]
    for j in range(1, DEVICES):
        total = total + sums[j]
    scale = jnp.sqrt(total)
    t = 0
    for out in (scale_query, scale_key, scale_value):
        for i in range(out.shape[0]):
            out[i : i + 1, :] = scale[:, t * LANES : (t + 1) * LANES]
            t += 1
    inverse = 1.0 / scale
    factors = [
        jnp.broadcast_to(inverse[:, t * LANES : (t + 1) * LANES], (16, LANES)) for t in range(tiles)
    ]

    def narrow(piece):
        start, count = PIECES[piece]

        def body(strip, carry):
            rows = pl.ds(pl.multiple_of(start + strip * 16, 16), 16)
            for t in range(tiles):
                lanes = pl.ds(t * LANES, LANES)
                blocks[me, rows, lanes] = (mixed[rows, lanes] * factors[t]).astype(jnp.bfloat16)
            return carry

        lax.fori_loop(0, count // 16, body, 0, unroll=2)

    up, down, across, sibling = (0, 1), (0, 3), (1, 0), None
    rows_sent = [0]

    def piece_copy(block, piece, target):
        rows = pl.ds(*PIECES[piece])
        if target is sibling:
            recv = sibling_sem.at[0]
            goal = device(0, 0, 1)
        else:
            recv = recv_sem.at[(block[0] - target[0]) % 2 * 4 + (block[1] - target[1]) % 4, piece]
            goal = device(*target)
        return remote(blocks.at[device(*block), rows, :], send_sem.at[0], recv, rows=goal)

    def send(block, piece, target):
        piece_copy(block, piece, target).start()
        rows_sent[0] += PIECES[piece][1]

    def arrived(block, piece):
        wait_bytes(
            blocks.at[device(*block), pl.ds(*PIECES[piece]), :],
            recv_sem.at[block[0] * 4 + block[1], piece],
        )

    own = (0, 0)
    narrow(0)
    send(own, 0, up)
    narrow(1)
    send(own, 1, down)
    send(own, 1, up)
    send(own, 0, down)
    narrow(2)
    send(own, 2, across)
    send(own, 2, up)
    narrow(3)
    send(own, 3, down)
    send(own, 3, across)
    send(own, 3, up)
    send(own, 2, down)
    send(own, 0, across)
    send(own, 1, across)
    for piece in range(4):
        send(own, piece, sibling)

    below, above, far = (0, 3), (0, 1), (0, 2)
    side, side_below, side_above, side_far = (1, 0), (1, 3), (1, 1), (1, 2)
    for block, piece, targets in (
        (below, 0, (up, across)),
        (above, 1, (down, across)),
        (side, 2, (up,)),
        (below, 1, (across,)),
        (above, 0, (across,)),
        (side, 3, (down, up)),
        (side, None, ()),
        (below, 2, (up,)),
        (above, 3, (down,)),
        (side, 0, ()),
        (below, 3, ()),
        (above, 2, ()),
        (side, 1, ()),
    ):
        if piece is None:
            send(side, 2, down)
            continue
        arrived(block, piece)
        for target in targets + (sibling,):
            send(block, piece, target)

    for j in range(1, PEERS):

        @pl.when(place + j < PEERS)
        def _():
            image_copy(place + j, place).wait_recv()
            image_copy(place, place + j).start()

    for block, piece, targets in (
        (far, 0, (across,)),
        (far, 1, (across,)),
        (side_below, 0, ()),
        (side_above, 1, ()),
        (side_below, 2, (up,)),
        (side_above, 3, (down,)),
        (side_below, 1, ()),
    ):
        arrived(block, piece)
        for target in targets + (sibling,):
            send(block, piece, target)

    for j in range(1, PEERS):

        @pl.when(place + j >= PEERS)
        def _():
            image_copy(place + j - PEERS, place).wait_recv()

    image = norm_images[0]
    for j in range(1, PEERS):
        image = image + norm_images[j]
    norm_pairs[me] = image
    for j in range(1, DEVICES):
        remote(
            norm_pairs.at[me], pair_sem.at[0], pair_sem.at[1], rows=lax.rem(me + j, DEVICES)
        ).start()

    for block, piece in (
        (side_below, 3),
        (side_above, 2),
        (side_above, 0),
        (far, 2),
        (far, 3),
        (side_far, 0),
    ):
        arrived(block, piece)
        send(block, piece, sibling)

    wait_bytes(norm_pairs.at[pl.ds(0, DEVICES - 1)], pair_sem.at[1])
    for j in range(DEVICES // 2):
        norm_all[pl.ds(7 * j, 8), :] = norm_pairs[2 * j] + norm_pairs[2 * j + 1]
    serve[...] = norm_all[pl.ds(0, NORM), :].astype(serve.dtype)
    wait_bytes(sums.at[pl.ds(0, DEVICES - 1)], sum_sem.at[0])
    wait_bytes(norm_images.at[pl.ds(0, PEERS - 1)], image_send.at[0])
    wait_bytes(norm_pairs.at[pl.ds(0, DEVICES - 1)], pair_sem.at[0])

    for block, piece in ((side_far, 1), (side_far, 2), (side_far, 3)):
        arrived(block, piece)
        send(block, piece, sibling)

    wait_bytes(blocks.at[pl.ds(0, DEVICES // 2)], sibling_sem.at[0])
    assert rows_sent[0] % depth == 0
    wait_bytes(blocks.at[pl.ds(0, rows_sent[0] // depth)], send_sem.at[0])


def write_kernel(
    blocks,
    scale_query,
    scale_key,
    scale_value,
    serve,
    query,
    key,
    value,
    query_scale,
    key_scale,
    value_scale,
    gains,
    sem,
    small_sem,
):
    depth = blocks.shape[1]
    outs = (query, key, value)
    for b in range(DEVICES):
        at = 0
        for n, out in enumerate(outs):
            pltpu.make_async_copy(
                blocks.at[b, :, pl.ds(at, out.shape[1])],
                out.at[pl.ds(b * depth, depth), :],
                sem.at[n],
            ).start()
            at += out.shape[1]
    small = (
        (scale_query, query_scale),
        (scale_key, key_scale),
        (scale_value, value_scale),
        (serve, gains),
    )
    for i, (source, target) in enumerate(small):
        pltpu.make_async_copy(source, target, small_sem.at[i]).start()
    for n, out in enumerate(outs):
        pltpu.make_async_copy(out, out, sem.at[n]).wait()
    for i, (source, target) in enumerate(small):
        pltpu.make_async_copy(source, target, small_sem.at[i]).wait()


def shards(
    one_query,
    other_query,
    one_key,
    other_key,
    one_value,
    other_value,
    mix_share,
    norm_train,
    norm_step,
):
    f32, bf16 = jnp.float32, jnp.bfloat16
    depth, queries = one_query.shape
    keys = one_key.shape[1]
    wide = queries + 2 * keys
    tall = -(-depth // LANES) * LANES
    dma = pltpu.SemaphoreType.DMA
    hbm, vmem = pl.BlockSpec(memory_space=pltpu.HBM), pl.BlockSpec(memory_space=pltpu.VMEM)
    blocks, scale_query, scale_key, scale_value, serve = pl.pallas_call(
        gather_kernel,
        out_shape=(
            pltpu.VMEM((DEVICES, depth, wide), bf16),
            pltpu.VMEM((queries // LANES, LANES), f32),
            pltpu.VMEM((keys // LANES, LANES), f32),
            pltpu.VMEM((keys // LANES, LANES), f32),
            pltpu.VMEM((NORM, LANES), bf16),
        ),
        in_specs=[hbm] * 9,
        out_specs=[vmem] * 5,
        scratch_shapes=[
            pltpu.VMEM((2, depth, wide), f32),
            pltpu.VMEM((depth, wide), f32),
            pltpu.VMEM((tall, LANES), f32),
            pltpu.VMEM((1, tall), f32),
            pltpu.VMEM((1, depth), f32),
            pltpu.VMEM((1, NORM), f32),
            pltpu.VMEM((1, NORM), f32),
            pltpu.VMEM((DEVICES, 1, wide), f32),
            pltpu.VMEM((1, LANES), f32),
            pltpu.VMEM((PEERS, 8, LANES), f32),
            pltpu.VMEM((DEVICES, 8, LANES), f32),
            pltpu.VMEM((64, LANES), f32),
            dma((LOADS,)),
            dma((3,)),
            dma((1,)),
            dma((8, 4)),
            dma((1,)),
            dma((2,)),
            dma((1,)),
            dma((PEERS,)),
            dma((2,)),
        ],
        compiler_params=pltpu.CompilerParams(
            collective_id=0, has_side_effects=True, vmem_limit_bytes=48 * 1024 * 1024
        ),
        name="gather",
    )(
        one_query,
        other_query,
        one_key,
        other_key,
        one_value,
        other_value,
        mix_share.reshape(1, depth),
        norm_train.reshape(1, NORM),
        norm_step.reshape(1, NORM),
    )
    finals = pl.pallas_call(
        write_kernel,
        out_shape=(
            jax.ShapeDtypeStruct((DEVICES * depth, queries), bf16),
            jax.ShapeDtypeStruct((DEVICES * depth, keys), bf16),
            jax.ShapeDtypeStruct((DEVICES * depth, keys), bf16),
            jax.ShapeDtypeStruct((queries // LANES, LANES), f32),
            jax.ShapeDtypeStruct((keys // LANES, LANES), f32),
            jax.ShapeDtypeStruct((keys // LANES, LANES), f32),
            jax.ShapeDtypeStruct((NORM, LANES), bf16),
        ),
        in_specs=[vmem] * 5,
        out_specs=[hbm] * 7,
        scratch_shapes=[dma((3,)), dma((4,))],
        compiler_params=pltpu.CompilerParams(vmem_limit_bytes=1024 * 1024),
        name="write",
    )(blocks, scale_query, scale_key, scale_value, serve)
    return finals[:3] + tuple(a.reshape(-1) for a in finals[3:])


def solution(mesh):
    in_specs = (
        P("rows", "width"),
        P("rows", "width"),
        P("rows", "width"),
        P("rows", "width"),
        P("rows", "width"),
        P("rows", "width"),
        P("rows"),
        P(("rows", "width")),
        P(("rows", "width")),
    )
    out_specs = (
        P(None, "width"),
        P(None, "width"),
        P(None, "width"),
        P("width"),
        P("width"),
        P("width"),
        P(),
    )
    return jax.shard_map(shards, mesh=mesh, in_specs=in_specs, out_specs=out_specs, check_vma=False)
```

time: 79.4 us -> 75.1 us (0.946)
  Pallas kernels: 78.6 us -> 74.3 us
    pallas_call x1, Pallas kernels: 72.4 us -> 68.5 us  [shards(): pl.pallas_call(gather_kernel, out_shape=(pltpu.VMEM((DEVICES, depth, wide...]
where the time goes in v2:
time: 75.1 us; the launch traced here: 74.9 us
  Pallas kernels  74.3 us (99%)
    pallas_call x1, Pallas kernels, shards(): pl.pallas_call(gather_kernel, out_shape=(pltpu.VMEM((DEVICES, depth, wide...  68.5 us
    pallas_call x1, Pallas kernels, shards(): pl.pallas_call(write_kernel, out_shape=(jax.ShapeDtypeStruct((DEVICES * d...  5.79 us

profile of v2, /device:TPU:1, one launch (start us, length us, event | category | flops | bytes accessed | tf_op | source)
XLA Modules:
  0.0 74.9 jit_solution(3983481383398902745)
XLA Ops:
  0.6 68.5 %gather.1 = (bf16[16,448,1152]{2,1,0:T(8,128)(2,1)S(1)}, f32[7,128]{1,0:T(8,128)S(1)}, f32[1,128]{1,0:T(1,128)S(1)}, f32[1,128]{1,0:T(1,128)S(1)}, bf16[56,128]{1,0:T(8,128)(2,1)S(1)}) custom-call(f32[448,896]{1,0:T(8,128)} %one_query.1, f32[448,896]{1,0:T(8,128)} %other_query.1, f32[448,128]{1,0:T(8,128)} %one_key.1, f32[448,128]{1,0:T(8,128)} %other_key.1, ...), custom_call_target="tpu_custom_call" | custom-call | tf_op jit(solution)/shard_map/gather/pallas_call | solution.py:377
  69.1 5.8 %write.1 = (bf16[7168,896]{1,0:T(8,128)(2,1)}, bf16[7168,128]{1,0:T(8,128)(2,1)}, bf16[7168,128]{1,0:T(8,128)(2,1)}, f32[7,128]{1,0:T(8,128)}, f32[1,128]{1,0:T(...) custom-call(bf16[16,448,1152]{2,1,0:T(8,128)(2,1)S(1)} %get-tuple-element.19.blocks, ...), custom_call_target="tpu_custom_call" | custom-call | tf_op jit(solution)/shard_map/write/pallas_call | solution.py:426

commit v3 on v2

--- a/solution.py
+++ b/solution.py
@@ -208,7 +208,13 @@
             recv_sem.at[block[0] * 4 + block[1], piece],
         )
 
-    own = (0, 0)
+    def pass_on(block, piece, *targets):
+        arrived(block, piece)
+        for target in targets + (sibling,):
+            send(block, piece, target)
+
+    own, below, above, far = (0, 0), (0, 3), (0, 1), (0, 2)
+    side, side_below, side_above, side_far = (1, 0), (1, 3), (1, 1), (1, 2)
     narrow(0)
     send(own, 0, up)
     narrow(1)
@@ -223,35 +229,10 @@
     send(own, 3, across)
     send(own, 3, up)
     send(own, 2, down)
-    send(own, 0, across)
-    send(own, 1, across)
     for piece in range(4):
         send(own, piece, sibling)
 
-    below, above, far = (0, 3), (0, 1), (0, 2)
-    side, side_below, side_above, side_far = (1, 0), (1, 3), (1, 1), (1, 2)
-    for block, piece, targets in (
-        (below, 0, (up, across)),
-        (above, 1, (down, across)),
-        (side, 2, (up,)),
-        (below, 1, (across,)),
-        (above, 0, (across,)),
-        (side, 3, (down, up)),
-        (side, None, ()),
-        (below, 2, (up,)),
-        (above, 3, (down,)),
-        (side, 0, ()),
-        (below, 3, ()),
-        (above, 2, ()),
-        (side, 1, ()),
-    ):
-        if piece is None:
-            send(side, 2, down)
-            continue
-        arrived(block, piece)
-        for target in targets + (sibling,):
-            send(block, piece, target)
-
+    pass_on(below, 0, up, across)
     for j in range(1, PEERS):
 
         @pl.when(place + j < PEERS)
@@ -259,19 +240,17 @@
             image_copy(place + j, place).wait_recv()
             image_copy(place, place + j).start()
 
-    for block, piece, targets in (
-        (far, 0, (across,)),
-        (far, 1, (across,)),
-        (side_below, 0, ()),
-        (side_above, 1, ()),
-        (side_below, 2, (up,)),
-        (side_above, 3, (down,)),
-        (side_below, 1, ()),
-    ):
-        arrived(block, piece)
-        for target in targets + (sibling,):
-            send(block, piece, target)
-
+    send(own, 0, across)
+    send(own, 1, across)
+    pass_on(above, 1, down, across)
+    pass_on(side, 2, up)
+    pass_on(below, 1, across)
+    pass_on(above, 0, across)
+    pass_on(side, 3, down, up)
+    send(side, 2, down)
+    pass_on(below, 2, up)
+    pass_on(above, 3, down)
+    pass_on(side, 0)
     for j in range(1, PEERS):
 
         @pl.when(place + j >= PEERS)
@@ -287,16 +266,25 @@
             norm_pairs.at[me], pair_sem.at[0], pair_sem.at[1], rows=lax.rem(me + j, DEVICES)
         ).start()
 
-    for block, piece in (
-        (side_below, 3),
-        (side_above, 2),
-        (side_above, 0),
-        (far, 2),
-        (far, 3),
-        (side_far, 0),
-    ):
-        arrived(block, piece)
-        send(block, piece, sibling)
+    pass_on(below, 3)
+    pass_on(above, 2)
+    pass_on(side, 1)
+    pass_on(far, 0, across)
+    pass_on(far, 1, across)
+    pass_on(side_below, 0)
+    pass_on(side_above, 1)
+    pass_on(side_below, 2, up)
+    pass_on(side_above, 3, down)
+    pass_on(side_below, 1)
+    pass_on(side_below, 3)
+    pass_on(side_above, 2)
+    pass_on(side_above, 0)
+    pass_on(far, 2)
+    pass_on(far, 3)
+    pass_on(side_far, 0)
+    pass_on(side_far, 1)
+    pass_on(side_far, 2)
+    pass_on(side_far, 3)
 
     wait_bytes(norm_pairs.at[pl.ds(0, DEVICES - 1)], pair_sem.at[1])
     for j in range(DEVICES // 2):
@@ -305,10 +293,6 @@
     wait_bytes(sums.at[pl.ds(0, DEVICES - 1)], sum_sem.at[0])
     wait_bytes(norm_images.at[pl.ds(0, PEERS - 1)], image_send.at[0])
     wait_bytes(norm_pairs.at[pl.ds(0, DEVICES - 1)], pair_sem.at[0])
-
-    for block, piece in ((side_far, 1), (side_far, 2), (side_far, 3)):
-        arrived(block, piece)
-        send(block, piece, sibling)
 
     wait_bytes(blocks.at[pl.ds(0, DEVICES // 2)], sibling_sem.at[0])
     assert rows_sent[0] % depth == 0

time: 75.1 us -> 74 us (0.985)
  Pallas kernels: 74.3 us -> 73.2 us
    pallas_call x1, Pallas kernels: 68.5 us -> 67.4 us  [shards(): pl.pallas_call(gather_kernel, out_shape=(pltpu.VMEM((DEVICES, depth, wide...]
where the time goes in v3:
time: 74 us; the launch traced here: 73.9 us
  Pallas kernels  73.2 us (99%)
    pallas_call x1, Pallas kernels, shards(): pl.pallas_call(gather_kernel, out_shape=(pltpu.VMEM((DEVICES, depth, wide...  67.4 us
    pallas_call x1, Pallas kernels, shards(): pl.pallas_call(write_kernel, out_shape=(jax.ShapeDtypeStruct((DEVICES * d...  5.79 us

profile of v3, /device:TPU:1, one launch (start us, length us, event | category | flops | bytes accessed | tf_op | source)
XLA Modules:
  0.0 73.9 jit_solution(1925542311580601415)
XLA Ops:
  0.6 67.4 %gather.1 = (bf16[16,448,1152]{2,1,0:T(8,128)(2,1)S(1)}, f32[7,128]{1,0:T(8,128)S(1)}, f32[1,128]{1,0:T(1,128)S(1)}, f32[1,128]{1,0:T(1,128)S(1)}, bf16[56,128]{1,0:T(8,128)(2,1)S(1)}) custom-call(f32[448,896]{1,0:T(8,128)} %one_query.1, f32[448,896]{1,0:T(8,128)} %other_query.1, f32[448,128]{1,0:T(8,128)} %one_key.1, f32[448,128]{1,0:T(8,128)} %other_key.1, ...), custom_call_target="tpu_custom_call" | custom-call | tf_op jit(solution)/shard_map/gather/pallas_call | solution.py:361
  68.1 5.8 %write.1 = (bf16[7168,896]{1,0:T(8,128)(2,1)}, bf16[7168,128]{1,0:T(8,128)(2,1)}, bf16[7168,128]{1,0:T(8,128)(2,1)}, f32[7,128]{1,0:T(8,128)}, f32[1,128]{1,0:T(...) custom-call(bf16[16,448,1152]{2,1,0:T(8,128)(2,1)S(1)} %get-tuple-element.19.blocks, ...), custom_call_target="tpu_custom_call" | custom-call | tf_op jit(solution)/shard_map/write/pallas_call | solution.py:410

commit v4 on v3

--- a/solution.py
+++ b/solution.py
@@ -11,7 +11,12 @@
 PEERS = 8
 NORM = 56
 
-PIECES = ((0, 96), (96, 96), (192, 128), (320, 128))
+LOW_UP, LOW_DOWN, HIGH_UP, HIGH_DOWN = (0, 104), (104, 96), (200, 120), (320, 128)
+EARLY = 40
+LAST_UP = ((200, 40), (240, 48), (288, 32))
+LAST_DOWN = ((320, 64), (384, 32), (416, 32))
+LAST_ACROSS = ((104, 64), (168, 32))
+ARRIVALS = 33
 LOADS = 4
 
 
@@ -42,6 +47,7 @@
     norm_images,
     norm_pairs,
     norm_all,
+    early,
     load_sem,
     small_sem,
     send_sem,
@@ -51,6 +57,8 @@
     image_send,
     image_recv,
     pair_sem,
+    early_send,
+    early_recv,
 ):
     depth, wide = mixed.shape
     tiles = wide // LANES
@@ -158,6 +166,18 @@
         def _():
             image_copy(place, place + j - PEERS).start()
 
+    up, down, across, sibling = (0, 1), (0, 3), (1, 0), None
+    early_parts = ((LOW_UP, up), (LOW_DOWN, down), (HIGH_UP, across))
+    for n, ((start, _), target) in enumerate(early_parts):
+        pltpu.make_async_remote_copy(
+            src_ref=mixed.at[pl.ds(start, EARLY), :],
+            dst_ref=early.at[n],
+            send_sem=early_send.at[0],
+            recv_sem=early_recv.at[n],
+            device_id={"rows": device(*target)},
+            device_id_type=MESH,
+        ).start()
+
     wait_bytes(sums.at[pl.ds(0, DEVICES - 1)], sum_sem.at[1])
     total = sums[0]
     for j in range(1, DEVICES):
@@ -170,69 +190,76 @@
             t += 1
     inverse = 1.0 / scale
     factors = [
-        jnp.broadcast_to(inverse[:, t * LANES : (t + 1) * LANES], (16, LANES)) for t in range(tiles)
+        jnp.broadcast_to(inverse[:, t * LANES : (t + 1) * LANES], (8, LANES)) for t in range(tiles)
     ]
 
-    def narrow(piece):
-        start, count = PIECES[piece]
-
+    def narrow(source, skip, block, start, count):
         def body(strip, carry):
-            rows = pl.ds(pl.multiple_of(start + strip * 16, 16), 16)
+            here = pl.ds(pl.multiple_of(skip + strip * 8, 8), 8)
+            there = pl.ds(pl.multiple_of(start + strip * 8, 8), 8)
             for t in range(tiles):
                 lanes = pl.ds(t * LANES, LANES)
-                blocks[me, rows, lanes] = (mixed[rows, lanes] * factors[t]).astype(jnp.bfloat16)
+                blocks[block, there, lanes] = (source[here, lanes] * factors[t]).astype(jnp.bfloat16)
             return carry
 
-        lax.fori_loop(0, count // 16, body, 0, unroll=2)
-
-    up, down, across, sibling = (0, 1), (0, 3), (1, 0), None
+        lax.fori_loop(0, count // 8, body, 0, unroll=4)
+
     rows_sent = [0]
-
-    def piece_copy(block, piece, target):
-        rows = pl.ds(*PIECES[piece])
+    places = {}
+
+    def arrival(block, part):
+        return recv_sem.at[places.setdefault((block, part), len(places))]
+
+    def part_copy(block, part, target):
+        rows = pl.ds(*part)
         if target is sibling:
             recv = sibling_sem.at[0]
             goal = device(0, 0, 1)
         else:
-            recv = recv_sem.at[(block[0] - target[0]) % 2 * 4 + (block[1] - target[1]) % 4, piece]
+            recv = arrival(((block[0] - target[0]) % 2, (block[1] - target[1]) % 4), part)
             goal = device(*target)
         return remote(blocks.at[device(*block), rows, :], send_sem.at[0], recv, rows=goal)
 
-    def send(block, piece, target):
-        piece_copy(block, piece, target).start()
-        rows_sent[0] += PIECES[piece][1]
-
-    def arrived(block, piece):
-        wait_bytes(
-            blocks.at[device(*block), pl.ds(*PIECES[piece]), :],
-            recv_sem.at[block[0] * 4 + block[1], piece],
-        )
-
-    def pass_on(block, piece, *targets):
-        arrived(block, piece)
-        for target in targets + (sibling,):
-            send(block, piece, target)
+    def send(block, part, *targets):
+        for target in targets:
+            part_copy(block, part, target).start()
+            rows_sent[0] += part[1]
+
+    def arrived(block, part):
+        wait_bytes(blocks.at[device(*block), pl.ds(*part), :], arrival(block, part))
+
+    def pass_on(block, part, *targets):
+        arrived(block, part)
+        send(block, part, *targets, sibling)
+
+    def rest(part):
+        return part[0] + EARLY, part[1] - EARLY
 
     own, below, above, far = (0, 0), (0, 3), (0, 1), (0, 2)
     side, side_below, side_above, side_far = (1, 0), (1, 3), (1, 1), (1, 2)
-    narrow(0)
-    send(own, 0, up)
-    narrow(1)
-    send(own, 1, down)
-    send(own, 1, up)
-    send(own, 0, down)
-    narrow(2)
-    send(own, 2, across)
-    send(own, 2, up)
-    narrow(3)
-    send(own, 3, down)
-    send(own, 3, across)
-    send(own, 3, up)
-    send(own, 2, down)
-    for piece in range(4):
-        send(own, piece, sibling)
-
-    pass_on(below, 0, up, across)
+    for part in (LOW_UP, LOW_DOWN, HIGH_UP, HIGH_DOWN):
+        narrow(mixed, part[0], me, *part)
+        if part is LOW_UP:
+            send(own, rest(LOW_UP), up)
+        if part is LOW_DOWN:
+            send(own, rest(LOW_DOWN), down)
+            send(own, LOW_DOWN, up)
+            send(own, LOW_UP, down)
+        if part is HIGH_UP:
+            send(own, rest(HIGH_UP), across)
+            send(own, HIGH_UP, up)
+    send(own, HIGH_DOWN, down, across, up)
+    send(own, HIGH_UP, down)
+    for part in (LOW_UP, LOW_DOWN, HIGH_UP, HIGH_DOWN):
+        send(own, part, sibling)
+    for n, (block, ((start, _), _)) in enumerate(zip((below, above, side), early_parts)):
+        wait_bytes(early.at[n], early_recv.at[n])
+        narrow(early.at[n], 0, device(*block), start, EARLY)
+
+    arrived(below, rest(LOW_UP))
+    send(below, LOW_UP, up)
+    arrived(above, rest(LOW_DOWN))
+    send(above, LOW_DOWN, down)
     for j in range(1, PEERS):
 
         @pl.when(place + j < PEERS)
@@ -240,17 +267,19 @@
             image_copy(place + j, place).wait_recv()
             image_copy(place, place + j).start()
 
-    send(own, 0, across)
-    send(own, 1, across)
-    pass_on(above, 1, down, across)
-    pass_on(side, 2, up)
-    pass_on(below, 1, across)
-    pass_on(above, 0, across)
-    pass_on(side, 3, down, up)
-    send(side, 2, down)
-    pass_on(below, 2, up)
-    pass_on(above, 3, down)
-    pass_on(side, 0)
+    send(own, LOW_UP, across)
+    send(own, LOW_DOWN, across)
+    send(below, LOW_UP, across, sibling)
+    send(above, LOW_DOWN, across, sibling)
+    arrived(side, rest(HIGH_UP))
+    send(side, HIGH_UP, up, sibling)
+    pass_on(below, LOW_DOWN, across)
+    pass_on(above, LOW_UP, across)
+    pass_on(side, HIGH_DOWN, down, up)
+    send(side, HIGH_UP, down)
+    pass_on(below, HIGH_UP, up)
+    pass_on(above, HIGH_DOWN, down)
+    pass_on(side, LOW_UP)
     for j in range(1, PEERS):
 
         @pl.when(place + j >= PEERS)
@@ -266,25 +295,39 @@
             norm_pairs.at[me], pair_sem.at[0], pair_sem.at[1], rows=lax.rem(me + j, DEVICES)
         ).start()
 
-    pass_on(below, 3)
-    pass_on(above, 2)
-    pass_on(side, 1)
-    pass_on(far, 0, across)
-    pass_on(far, 1, across)
-    pass_on(side_below, 0)
-    pass_on(side_above, 1)
-    pass_on(side_below, 2, up)
-    pass_on(side_above, 3, down)
-    pass_on(side_below, 1)
-    pass_on(side_below, 3)
-    pass_on(side_above, 2)
-    pass_on(side_above, 0)
-    pass_on(far, 2)
-    pass_on(far, 3)
-    pass_on(side_far, 0)
-    pass_on(side_far, 1)
-    pass_on(side_far, 2)
-    pass_on(side_far, 3)
+    pass_on(below, HIGH_DOWN)
+    pass_on(above, HIGH_UP)
+    pass_on(side, LOW_DOWN)
+    pass_on(far, LOW_UP, across)
+    arrived(far, LOW_DOWN)
+    send(far, LOW_DOWN, sibling)
+    for part in LAST_ACROSS:
+        send(far, part, across)
+    pass_on(side_below, LOW_UP)
+    pass_on(side_above, LOW_DOWN)
+    arrived(side_below, HIGH_UP)
+    for part in LAST_UP:
+        send(side_below, part, up)
+    send(side_below, HIGH_UP, sibling)
+    arrived(side_above, HIGH_DOWN)
+    for part in LAST_DOWN:
+        send(side_above, part, down)
+    send(side_above, HIGH_DOWN, sibling)
+    pass_on(side_below, LOW_DOWN)
+    pass_on(side_below, HIGH_DOWN)
+    pass_on(side_above, HIGH_UP)
+    pass_on(side_above, LOW_UP)
+    pass_on(far, HIGH_UP)
+    pass_on(far, HIGH_DOWN)
+    pass_on(side_far, LOW_UP)
+    for up_part, down_part in zip(LAST_UP[:2], LAST_DOWN[:2]):
+        pass_on(side_far, up_part)
+        pass_on(side_far, down_part)
+    pass_on(side_far, LAST_ACROSS[0])
+    pass_on(side_far, LAST_UP[2])
+    pass_on(side_far, LAST_DOWN[2])
+    pass_on(side_far, LAST_ACROSS[1])
+    assert len(places) == ARRIVALS
 
     wait_bytes(norm_pairs.at[pl.ds(0, DEVICES - 1)], pair_sem.at[1])
     for j in range(DEVICES // 2):
@@ -294,9 +337,11 @@
     wait_bytes(norm_images.at[pl.ds(0, PEERS - 1)], image_send.at[0])
     wait_bytes(norm_pairs.at[pl.ds(0, DEVICES - 1)], pair_sem.at[0])
 
+    wait_bytes(early, early_send.at[0])
     wait_bytes(blocks.at[pl.ds(0, DEVICES // 2)], sibling_sem.at[0])
-    assert rows_sent[0] % depth == 0
-    wait_bytes(blocks.at[pl.ds(0, rows_sent[0] // depth)], send_sem.at[0])
+    count = -(-rows_sent[0] // depth)
+    assert rows_sent[0] % (count * 8) == 0
+    wait_bytes(blocks.at[pl.ds(0, count), pl.ds(0, rows_sent[0] // count), :], send_sem.at[0])
 
 
 def write_kernel(
@@ -382,15 +427,18 @@
             pltpu.VMEM((PEERS, 8, LANES), f32),
             pltpu.VMEM((DEVICES, 8, LANES), f32),
             pltpu.VMEM((64, LANES), f32),
+            pltpu.VMEM((3, EARLY, wide), f32),
             dma((LOADS,)),
             dma((3,)),
             dma((1,)),
-            dma((8, 4)),
+            dma((ARRIVALS,)),
             dma((1,)),
             dma((2,)),
             dma((1,)),
             dma((PEERS,)),
             dma((2,)),
+            dma((1,)),
+            dma((3,)),
         ],
         compiler_params=pltpu.CompilerParams(
             collective_id=0, has_side_effects=True, vmem_limit_bytes=48 * 1024 * 1024

time: 74 us -> 71.3 us (0.964)
  Pallas kernels: 73.2 us -> 70.6 us
    pallas_call x1, Pallas kernels: 67.4 us -> 64.8 us  [shards(): pl.pallas_call(gather_kernel, out_shape=(pltpu.VMEM((DEVICES, depth, wide...]
where the time goes in v4:
time: 71.3 us; the launch traced here: 71.2 us
  Pallas kernels  70.6 us (99%)
    pallas_call x1, Pallas kernels, shards(): pl.pallas_call(gather_kernel, out_shape=(pltpu.VMEM((DEVICES, depth, wide...  64.8 us
    pallas_call x1, Pallas kernels, shards(): pl.pallas_call(write_kernel, out_shape=(jax.ShapeDtypeStruct((DEVICES * d...  5.79 us

profile of v4, /device:TPU:1, one launch (start us, length us, event | category | flops | bytes accessed | tf_op | source)
XLA Modules:
  0.0 71.2 jit_solution(5419706690393535234)
XLA Ops:
  0.6 64.8 %gather.1 = (bf16[16,448,1152]{2,1,0:T(8,128)(2,1)S(1)}, f32[7,128]{1,0:T(8,128)S(1)}, f32[1,128]{1,0:T(1,128)S(1)}, f32[1,128]{1,0:T(1,128)S(1)}, bf16[56,128]{1,0:T(8,128)(2,1)S(1)}) custom-call(f32[448,896]{1,0:T(8,128)} %one_query.1, f32[448,896]{1,0:T(8,128)} %other_query.1, f32[448,128]{1,0:T(8,128)} %one_key.1, f32[448,128]{1,0:T(8,128)} %other_key.1, ...), custom_call_target="tpu_custom_call" | custom-call | tf_op jit(solution)/shard_map/gather/pallas_call | solution.py:406
  65.4 5.8 %write.1 = (bf16[7168,896]{1,0:T(8,128)(2,1)}, bf16[7168,128]{1,0:T(8,128)(2,1)}, bf16[7168,128]{1,0:T(8,128)(2,1)}, f32[7,128]{1,0:T(8,128)}, f32[1,128]{1,0:T(...) custom-call(bf16[16,448,1152]{2,1,0:T(8,128)(2,1)S(1)} %get-tuple-element.19.blocks, ...), custom_call_target="tpu_custom_call" | custom-call | tf_op jit(solution)/shard_map/write/pallas_call | solution.py:458

commit v5 on v4

--- a/solution.py
+++ b/solution.py
@@ -8,6 +8,7 @@
 MESH = pl.DeviceIdType.MESH
 LANES = 128
 DEVICES = 16
+CHIPS = 8
 PEERS = 8
 NORM = 56
 
@@ -43,9 +44,9 @@
     train_here,
     step_here,
     sums,
-    norm_row,
+    halves,
+    norm_rows,
     norm_images,
-    norm_pairs,
     norm_all,
     early,
     load_sem,
@@ -54,9 +55,11 @@
     recv_sem,
     sibling_sem,
     sum_sem,
-    image_send,
-    image_recv,
-    pair_sem,
+    half_sem,
+    row_send,
+    row_recv,
+    image_sem,
+    both_sem,
     early_send,
     early_recv,
 ):
@@ -67,6 +70,7 @@
     core = lax.rem(me, 2)
     y = lax.rem(lax.div(me, 2), 4)
     z = lax.div(me, 8)
+    chip = lax.div(me, 2)
 
     def device(dz, dy, other=0):
         return lax.rem(z + dz, 2) * 8 + lax.rem(y + dy, 4) * 2 + lax.rem(core + other, 2)
@@ -84,12 +88,9 @@
     def wait_bytes(ref, sem):
         pltpu.make_async_copy(ref, ref, sem).wait()
 
-    for i, (source, target) in enumerate(
-        ((mix, mix_here), (train, train_here), (step, step_here))
-    ):
-        pltpu.make_async_copy(source, target, small_sem.at[i]).start()
     chunk = depth // LOADS
-    for i in range(LOADS):
+
+    def load(i):
         rows = pl.ds(i * chunk, chunk)
         at = 0
         for pair in ((one_query, other_query), (one_key, other_key), (one_value, other_value)):
@@ -100,6 +101,11 @@
                 ).start()
             at += pair[0].shape[1]
 
+    load(0)
+    for i, (source, target) in enumerate(
+        ((mix, mix_here), (train, train_here), (step, step_here))
+    ):
+        pltpu.make_async_copy(source, target, small_sem.at[i]).start()
     barrier = pltpu.get_barrier_semaphore()
     for j in range(1, DEVICES):
         pl.semaphore_signal(
@@ -113,6 +119,9 @@
                 barrier, inc=1, device_id={"width": place + j}, device_id_type=MESH
             )
 
+    for i in range(1, LOADS):
+        load(i)
+
     for i, target in enumerate((mix_here, train_here, step_here)):
         wait_bytes(target, small_sem.at[i])
 
@@ -122,16 +131,8 @@
         row = share_row[:, pl.ds(i * LANES, LANES)]
         shares[pl.ds(i * LANES, LANES), :] = jnp.broadcast_to(row, (LANES, LANES)).T
 
-    norm_row[...] = jnp.zeros_like(norm_row)
-    norm_row[:, pl.ds(0, NORM)] = train_here[...] + step_here[...]
-    first = (core * PEERS + place) * NORM
-    gains = jnp.broadcast_to(norm_row[...], (8, LANES))
-    gains = pltpu.roll(gains, lax.rem(first, LANES), 1)
-    flat = lax.broadcasted_iota(jnp.int32, (8, LANES), 0) * LANES + lax.broadcasted_iota(
-        jnp.int32, (8, LANES), 1
-    )
-    inside = (flat >= first) & (flat < first + NORM)
-    norm_images[place] = jnp.where(inside, gains, 0.0)
+    norm_rows[place] = jnp.zeros((1, LANES), jnp.float32)
+    norm_rows[place, :, pl.ds(0, NORM)] = train_here[...] + step_here[...]
 
     def mix_rows(strip, partial):
         rows = pl.ds(pl.multiple_of(strip * 8, 8), 8)
@@ -150,21 +151,22 @@
         wait_bytes(both.at[:, pl.ds(i * chunk, chunk), :], load_sem.at[i])
         partial = lax.fori_loop(i * chunk // 8, (i + 1) * chunk // 8, mix_rows, partial, unroll=2)
     for t in range(tiles):
-        sums[me, :, pl.ds(t * LANES, LANES)] = jnp.sum(partial[t], axis=0, keepdims=True)
+        sums[chip, :, pl.ds(t * LANES, LANES)] = jnp.sum(partial[t], axis=0, keepdims=True)
 
     pl.semaphore_wait(barrier, DEVICES - 1 + place)
 
-    for j in range(1, DEVICES):
-        remote(sums.at[me], sum_sem.at[0], sum_sem.at[1], rows=lax.rem(me + j, DEVICES)).start()
-
-    def image_copy(source, target):
-        return remote(norm_images.at[source], image_send.at[0], image_recv.at[source], width=target)
+    others = ((1, 2), (1, 1), (1, 3), (0, 2), (1, 0), (0, 1), (0, 3))
+    for dz, dy in others:
+        remote(sums.at[chip], sum_sem.at[0], sum_sem.at[1], rows=device(dz, dy)).start()
+
+    def row_copy(source, target):
+        return remote(norm_rows.at[source], row_send.at[0], row_recv.at[source], width=target)
 
     for j in range(1, PEERS):
 
         @pl.when(place + j >= PEERS)
         def _():
-            image_copy(place, place + j - PEERS).start()
+            row_copy(place, place + j - PEERS).start()
 
     up, down, across, sibling = (0, 1), (0, 3), (1, 0), None
     early_parts = ((LOW_UP, up), (LOW_DOWN, down), (HIGH_UP, across))
@@ -178,10 +180,14 @@
             device_id_type=MESH,
         ).start()
 
-    wait_bytes(sums.at[pl.ds(0, DEVICES - 1)], sum_sem.at[1])
-    total = sums[0]
-    for j in range(1, DEVICES):
-        total = total + sums[j]
+    wait_bytes(sums.at[pl.ds(0, CHIPS - 1)], sum_sem.at[1])
+    half = sums[0]
+    for j in range(1, CHIPS):
+        half = half + sums[j]
+    halves[core] = half
+    remote(halves.at[core], half_sem.at[0], half_sem.at[1], rows=device(0, 0, 1)).start()
+    wait_bytes(halves.at[0], half_sem.at[1])
+    total = halves[0] + halves[1]
     scale = jnp.sqrt(total)
     t = 0
     for out in (scale_query, scale_key, scale_value):
@@ -213,17 +219,25 @@
     def part_copy(block, part, target):
         rows = pl.ds(*part)
         if target is sibling:
-            recv = sibling_sem.at[0]
-            goal = device(0, 0, 1)
-        else:
-            recv = arrival(((block[0] - target[0]) % 2, (block[1] - target[1]) % 4), part)
-            goal = device(*target)
-        return remote(blocks.at[device(*block), rows, :], send_sem.at[0], recv, rows=goal)
+            return remote(
+                blocks.at[device(*block), rows, :],
+                send_sem.at[1],
+                sibling_sem.at[0],
+                rows=device(0, 0, 1),
+            )
+        there = ((block[0] - target[0]) % 2, (block[1] - target[1]) % 4)
+        return remote(
+            blocks.at[device(*block), rows, :],
+            send_sem.at[0],
+            arrival(there, part),
+            rows=device(*target),
+        )
 
     def send(block, part, *targets):
         for target in targets:
             part_copy(block, part, target).start()
-            rows_sent[0] += part[1]
+            if target is not sibling:
+                rows_sent[0] += part[1]
 
     def arrived(block, part):
         wait_bytes(blocks.at[device(*block), pl.ds(*part), :], arrival(block, part))
@@ -264,8 +278,8 @@
 
         @pl.when(place + j < PEERS)
         def _():
-            image_copy(place + j, place).wait_recv()
-            image_copy(place, place + j).start()
+            row_copy(place + j, place).wait_recv()
+            row_copy(place, place + j).start()
 
     send(own, LOW_UP, across)
     send(own, LOW_DOWN, across)
@@ -284,15 +298,20 @@
 
         @pl.when(place + j >= PEERS)
         def _():
-            image_copy(place + j - PEERS, place).wait_recv()
-
-    image = norm_images[0]
-    for j in range(1, PEERS):
-        image = image + norm_images[j]
-    norm_pairs[me] = image
-    for j in range(1, DEVICES):
+            row_copy(place + j - PEERS, place).wait_recv()
+
+    flat = lax.broadcasted_iota(jnp.int32, (8, LANES), 0) * LANES + lax.broadcasted_iota(
+        jnp.int32, (8, LANES), 1
+    )
+    image = jnp.zeros((8, LANES), jnp.float32)
+    for j in range(PEERS):
+        first = (core * PEERS + j) * NORM
+        gains = pltpu.roll(jnp.broadcast_to(norm_rows[j], (8, LANES)), lax.rem(first, LANES), 1)
+        image = jnp.where((flat >= first) & (flat < first + NORM), gains, image)
+    norm_images[core, chip] = image.astype(jnp.bfloat16)
+    for dz, dy in others:
         remote(
-            norm_pairs.at[me], pair_sem.at[0], pair_sem.at[1], rows=lax.rem(me + j, DEVICES)
+            norm_images.at[core, chip], image_sem.at[0], image_sem.at[1], rows=device(dz, dy)
         ).start()
 
     pass_on(below, HIGH_DOWN)
@@ -319,6 +338,8 @@
     pass_on(side_above, LOW_UP)
     pass_on(far, HIGH_UP)
     pass_on(far, HIGH_DOWN)
+    wait_bytes(norm_images.at[0, pl.ds(0, CHIPS - 1)], image_sem.at[1])
+    remote(norm_images.at[core], both_sem.at[0], both_sem.at[1], rows=device(0, 0, 1)).start()
     pass_on(side_far, LOW_UP)
     for up_part, down_part in zip(LAST_UP[:2], LAST_DOWN[:2]):
         pass_on(side_far, up_part)
@@ -329,19 +350,23 @@
     pass_on(side_far, LAST_ACROSS[1])
     assert len(places) == ARRIVALS
 
-    wait_bytes(norm_pairs.at[pl.ds(0, DEVICES - 1)], pair_sem.at[1])
-    for j in range(DEVICES // 2):
-        norm_all[pl.ds(7 * j, 8), :] = norm_pairs[2 * j] + norm_pairs[2 * j + 1]
+    wait_bytes(norm_images.at[0], both_sem.at[1])
+    for j in range(CHIPS):
+        norm_all[pl.ds(7 * j, 8), :] = norm_images[0, j].astype(jnp.float32) + norm_images[
+            1, j
+        ].astype(jnp.float32)
     serve[...] = norm_all[pl.ds(0, NORM), :].astype(serve.dtype)
-    wait_bytes(sums.at[pl.ds(0, DEVICES - 1)], sum_sem.at[0])
-    wait_bytes(norm_images.at[pl.ds(0, PEERS - 1)], image_send.at[0])
-    wait_bytes(norm_pairs.at[pl.ds(0, DEVICES - 1)], pair_sem.at[0])
-
+    wait_bytes(sums.at[pl.ds(0, CHIPS - 1)], sum_sem.at[0])
+    wait_bytes(halves.at[0], half_sem.at[0])
+    wait_bytes(norm_rows.at[pl.ds(0, PEERS - 1)], row_send.at[0])
+    wait_bytes(norm_images.at[0, pl.ds(0, CHIPS - 1)], image_sem.at[0])
+    wait_bytes(norm_images.at[0], both_sem.at[0])
     wait_bytes(early, early_send.at[0])
     wait_bytes(blocks.at[pl.ds(0, DEVICES // 2)], sibling_sem.at[0])
-    count = -(-rows_sent[0] // depth)
-    assert rows_sent[0] % (count * 8) == 0
-    wait_bytes(blocks.at[pl.ds(0, count), pl.ds(0, rows_sent[0] // count), :], send_sem.at[0])
+    strips = rows_sent[0] // 8
+    count = next(n for n in range(1, DEVICES + 1) if strips % n == 0 and strips // n <= depth // 8)
+    wait_bytes(blocks.at[pl.ds(0, count), pl.ds(0, strips // count * 8), :], send_sem.at[0])
+    wait_bytes(blocks.at[pl.ds(0, DEVICES // 2)], send_sem.at[1])
 
 
 def write_kernel(
@@ -422,20 +447,22 @@
             pltpu.VMEM((1, depth), f32),
             pltpu.VMEM((1, NORM), f32),
             pltpu.VMEM((1, NORM), f32),
-            pltpu.VMEM((DEVICES, 1, wide), f32),
-            pltpu.VMEM((1, LANES), f32),
-            pltpu.VMEM((PEERS, 8, LANES), f32),
-            pltpu.VMEM((DEVICES, 8, LANES), f32),
+            pltpu.VMEM((CHIPS, 1, wide), f32),
+            pltpu.VMEM((2, 1, wide), f32),
+            pltpu.VMEM((PEERS, 1, LANES), f32),
+            pltpu.VMEM((2, CHIPS, 8, LANES), bf16),
             pltpu.VMEM((64, LANES), f32),
             pltpu.VMEM((3, EARLY, wide), f32),
             dma((LOADS,)),
             dma((3,)),
-            dma((1,)),
+            dma((2,)),
             dma((ARRIVALS,)),
             dma((1,)),
             dma((2,)),
+            dma((2,)),
             dma((1,)),
             dma((PEERS,)),
+            dma((2,)),
             dma((2,)),
             dma((1,)),
             dma((3,)),

time: 71.3 us -> 70.1 us (0.983)
  Pallas kernels: 70.6 us -> 69.4 us
    pallas_call x1, Pallas kernels: 64.8 us -> 63.6 us  [shards(): pl.pallas_call(gather_kernel, out_shape=(pltpu.VMEM((DEVICES, depth, wide...]
where the time goes in v5:
time: 70.1 us; the launch traced here: 70 us
  Pallas kernels  69.4 us (99%)
    pallas_call x1, Pallas kernels, shards(): pl.pallas_call(gather_kernel, out_shape=(pltpu.VMEM((DEVICES, depth, wide...  63.6 us
    pallas_call x1, Pallas kernels, shards(): pl.pallas_call(write_kernel, out_shape=(jax.ShapeDtypeStruct((DEVICES * d...  5.79 us

profile of v5, /device:TPU:1, one launch (start us, length us, event | category | flops | bytes accessed | tf_op | source)
XLA Modules:
  0.0 70.0 jit_solution(11851790900367776146)
XLA Ops:
  0.6 63.6 %gather.1 = (bf16[16,448,1152]{2,1,0:T(8,128)(2,1)S(1)}, f32[7,128]{1,0:T(8,128)S(1)}, f32[1,128]{1,0:T(1,128)S(1)}, f32[1,128]{1,0:T(1,128)S(1)}, bf16[56,128]{1,0:T(8,128)(2,1)S(1)}) custom-call(f32[448,896]{1,0:T(8,128)} %one_query.1, f32[448,896]{1,0:T(8,128)} %other_query.1, f32[448,128]{1,0:T(8,128)} %one_key.1, f32[448,128]{1,0:T(8,128)} %other_key.1, ...), custom_call_target="tpu_custom_call" | custom-call | tf_op jit(solution)/shard_map/gather/pallas_call | solution.py:431
  64.2 5.8 %write.1 = (bf16[7168,896]{1,0:T(8,128)(2,1)}, bf16[7168,128]{1,0:T(8,128)(2,1)}, bf16[7168,128]{1,0:T(8,128)(2,1)}, f32[7,128]{1,0:T(8,128)}, f32[1,128]{1,0:T(...) custom-call(bf16[16,448,1152]{2,1,0:T(8,128)(2,1)S(1)} %get-tuple-element.19.blocks, ...), custom_call_target="tpu_custom_call" | custom-call | tf_op jit(solution)/shard_map/write/pallas_call | solution.py:485

commit v6 on v5

--- a/solution.py
+++ b/solution.py
@@ -14,10 +14,45 @@
 
 LOW_UP, LOW_DOWN, HIGH_UP, HIGH_DOWN = (0, 104), (104, 96), (200, 120), (320, 128)
 EARLY = 40
-LAST_UP = ((200, 40), (240, 48), (288, 32))
-LAST_DOWN = ((320, 64), (384, 32), (416, 32))
-LAST_ACROSS = ((104, 64), (168, 32))
-ARRIVALS = 33
+LAST_UP = ((200, 40), (240, 48), (288, 16))
+LAST_DOWN = ((320, 64), (384, 32), (416, 16))
+LAST_ACROSS = ((104, 64), (168, 16))
+LENT_UP, LENT_DOWN, LENT_ACROSS = (304, 16), (432, 16), (184, 16)
+
+
+def rest(part):
+    return part[0] + EARLY, part[1] - EARLY
+
+
+BELOW, ABOVE, FAR = (0, 3), (0, 1), (0, 2)
+SIDE, SIDE_BELOW, SIDE_ABOVE, SIDE_FAR = (1, 0), (1, 3), (1, 1), (1, 2)
+ARRIVALS = (
+    ((BELOW, rest(LOW_UP)), (ABOVE, rest(LOW_DOWN))),
+    ((SIDE, rest(HIGH_UP)),),
+    ((BELOW, LOW_DOWN), (ABOVE, LOW_UP)),
+    ((SIDE, HIGH_DOWN),),
+    ((BELOW, HIGH_UP), (ABOVE, HIGH_DOWN)),
+    ((BELOW, HIGH_DOWN), (ABOVE, HIGH_UP), (SIDE, LOW_UP), (SIDE, LOW_DOWN)),
+    ((FAR, LOW_UP), (FAR, LOW_DOWN)),
+    ((SIDE_BELOW, HIGH_UP), (SIDE_ABOVE, HIGH_DOWN)),
+    (
+        (SIDE_BELOW, LOW_UP),
+        (SIDE_BELOW, LOW_DOWN),
+        (SIDE_BELOW, HIGH_DOWN),
+        (SIDE_ABOVE, HIGH_UP),
+    ),
+    ((SIDE_ABOVE, LOW_UP), (SIDE_ABOVE, LOW_DOWN), (FAR, HIGH_UP), (FAR, HIGH_DOWN)),
+    ((SIDE_FAR, LOW_UP),),
+    ((SIDE_FAR, LAST_UP[0]), (SIDE_FAR, LAST_DOWN[0])),
+    ((SIDE_FAR, LAST_UP[1]), (SIDE_FAR, LAST_DOWN[1])),
+    ((SIDE_FAR, LAST_ACROSS[0]),),
+    ((SIDE_FAR, LAST_UP[2]), (SIDE_FAR, LAST_DOWN[2])),
+    ((SIDE_FAR, LAST_ACROSS[1]),),
+    ((SIDE_FAR, LENT_UP), (SIDE_FAR, LENT_DOWN)),
+    ((SIDE_FAR, LENT_ACROSS),),
+)
+OWN_LENT = len(ARRIVALS) - 2
+SIBLING_LENT = len(ARRIVALS)
 LOADS = 4
 
 
@@ -168,11 +203,11 @@
         def _():
             row_copy(place, place + j - PEERS).start()
 
-    up, down, across, sibling = (0, 1), (0, 3), (1, 0), None
+    up, down, across = (0, 1), (0, 3), (1, 0)
     early_parts = ((LOW_UP, up), (LOW_DOWN, down), (HIGH_UP, across))
-    for n, ((start, _), target) in enumerate(early_parts):
+    for n, (part, target) in enumerate(early_parts):
         pltpu.make_async_remote_copy(
-            src_ref=mixed.at[pl.ds(start, EARLY), :],
+            src_ref=mixed.at[pl.ds(part[0], EARLY), :],
             dst_ref=early.at[n],
             send_sem=early_send.at[0],
             recv_sem=early_recv.at[n],
@@ -210,47 +245,33 @@
 
         lax.fori_loop(0, count // 8, body, 0, unroll=4)
 
-    rows_sent = [0]
-    places = {}
-
-    def arrival(block, part):
-        return recv_sem.at[places.setdefault((block, part), len(places))]
-
-    def part_copy(block, part, target):
-        rows = pl.ds(*part)
-        if target is sibling:
-            return remote(
-                blocks.at[device(*block), rows, :],
-                send_sem.at[1],
-                sibling_sem.at[0],
-                rows=device(0, 0, 1),
-            )
-        there = ((block[0] - target[0]) % 2, (block[1] - target[1]) % 4)
-        return remote(
-            blocks.at[device(*block), rows, :],
-            send_sem.at[0],
-            arrival(there, part),
-            rows=device(*target),
-        )
+    rows_sent = {}
+
+    def start(source, part, send_by, recv, goal):
+        remote(
+            blocks.at[source, pl.ds(*part), :], send_sem.at[send_by], recv, rows=goal
+        ).start()
+        rows_sent[send_by] = rows_sent.get(send_by, 0) + part[1]
+
+    line_of = {arrival: n for n, line in enumerate(ARRIVALS) for arrival in line}
 
     def send(block, part, *targets):
         for target in targets:
-            part_copy(block, part, target).start()
-            if target is not sibling:
-                rows_sent[0] += part[1]
-
-    def arrived(block, part):
-        wait_bytes(blocks.at[device(*block), pl.ds(*part), :], arrival(block, part))
-
-    def pass_on(block, part, *targets):
-        arrived(block, part)
-        send(block, part, *targets, sibling)
-
-    def rest(part):
-        return part[0] + EARLY, part[1] - EARLY
-
-    own, below, above, far = (0, 0), (0, 3), (0, 1), (0, 2)
-    side, side_below, side_above, side_far = (1, 0), (1, 3), (1, 1), (1, 2)
+            line = line_of[((block[0] - target[0]) % 2, (block[1] - target[1]) % 4), part]
+            start(device(*block), part, 0, recv_sem.at[line], device(*target))
+
+    def share(block, part, recv=1):
+        start(device(*block), part, 1, sibling_sem.at[recv], device(0, 0, 1))
+
+    def wait_rows(count, sem):
+        strips = count // 8
+        n = next(n for n in range(1, DEVICES + 1) if strips % n == 0 and strips // n <= depth // 8)
+        wait_bytes(blocks.at[pl.ds(0, n), pl.ds(0, strips // n * 8), :], sem)
+
+    def arrived(line):
+        wait_rows(sum(part[1] for _, part in ARRIVALS[line]), recv_sem.at[line])
+
+    own = (0, 0)
     for part in (LOW_UP, LOW_DOWN, HIGH_UP, HIGH_DOWN):
         narrow(mixed, part[0], me, *part)
         if part is LOW_UP:
@@ -265,15 +286,14 @@
     send(own, HIGH_DOWN, down, across, up)
     send(own, HIGH_UP, down)
     for part in (LOW_UP, LOW_DOWN, HIGH_UP, HIGH_DOWN):
-        send(own, part, sibling)
-    for n, (block, ((start, _), _)) in enumerate(zip((below, above, side), early_parts)):
+        share(own, part, 0)
+    for n, (block, (part, _)) in enumerate(zip((BELOW, ABOVE, SIDE), early_parts)):
         wait_bytes(early.at[n], early_recv.at[n])
-        narrow(early.at[n], 0, device(*block), start, EARLY)
-
-    arrived(below, rest(LOW_UP))
-    send(below, LOW_UP, up)
-    arrived(above, rest(LOW_DOWN))
-    send(above, LOW_DOWN, down)
+        narrow(early.at[n], 0, device(*block), part[0], EARLY)
+
+    arrived(0)
+    send(BELOW, LOW_UP, up)
+    send(ABOVE, LOW_DOWN, down)
     for j in range(1, PEERS):
 
         @pl.when(place + j < PEERS)
@@ -283,17 +303,25 @@
 
     send(own, LOW_UP, across)
     send(own, LOW_DOWN, across)
-    send(below, LOW_UP, across, sibling)
-    send(above, LOW_DOWN, across, sibling)
-    arrived(side, rest(HIGH_UP))
-    send(side, HIGH_UP, up, sibling)
-    pass_on(below, LOW_DOWN, across)
-    pass_on(above, LOW_UP, across)
-    pass_on(side, HIGH_DOWN, down, up)
-    send(side, HIGH_UP, down)
-    pass_on(below, HIGH_UP, up)
-    pass_on(above, HIGH_DOWN, down)
-    pass_on(side, LOW_UP)
+    for block, part in ((BELOW, LOW_UP), (ABOVE, LOW_DOWN)):
+        send(block, part, across)
+        share(block, part)
+    arrived(1)
+    send(SIDE, HIGH_UP, up)
+    share(SIDE, HIGH_UP)
+    arrived(2)
+    for block, part in ARRIVALS[2]:
+        send(block, part, across)
+        share(block, part)
+    arrived(3)
+    send(SIDE, HIGH_DOWN, down, up)
+    send(SIDE, HIGH_UP, down)
+    share(SIDE, HIGH_DOWN)
+    arrived(4)
+    send(BELOW, HIGH_UP, up)
+    send(ABOVE, HIGH_DOWN, down)
+    for block, part in ARRIVALS[4]:
+        share(block, part)
     for j in range(1, PEERS):
 
         @pl.when(place + j >= PEERS)
@@ -314,41 +342,65 @@
             norm_images.at[core, chip], image_sem.at[0], image_sem.at[1], rows=device(dz, dy)
         ).start()
 
-    pass_on(below, HIGH_DOWN)
-    pass_on(above, HIGH_UP)
-    pass_on(side, LOW_DOWN)
-    pass_on(far, LOW_UP, across)
-    arrived(far, LOW_DOWN)
-    send(far, LOW_DOWN, sibling)
+    arrived(5)
+    for block, part in ARRIVALS[5]:
+        share(block, part, 0)
+
+    def lend(parts, line, lent):
+        @pl.when(core == 1)
+        def _():
+            for block, part, target in parts:
+                there = ((block[0] - target[0]) % 2, (block[1] - target[1]) % 4)
+                assert line_of[there, part] == line
+                start(device(*block), part, 2, recv_sem.at[line], device(*target))
+            wait_rows(lent[1], sibling_sem.at[lent[0]])
+            for block, part, target in parts:
+                recv = recv_sem.at[line - OWN_LENT + SIBLING_LENT]
+                start(device(*block, 1), part, 2, recv, device(*target))
+
+        @pl.when(core == 0)
+        def _():
+            wait_rows(lent[1], sibling_sem.at[lent[0]])
+
+    arrived(6)
+    send(FAR, LOW_UP, across)
     for part in LAST_ACROSS:
-        send(far, part, across)
-    pass_on(side_below, LOW_UP)
-    pass_on(side_above, LOW_DOWN)
-    arrived(side_below, HIGH_UP)
+        send(FAR, part, across)
+    share(FAR, LOW_DOWN, 3)
+    share(FAR, LOW_UP)
+    arrived(7)
     for part in LAST_UP:
-        send(side_below, part, up)
-    send(side_below, HIGH_UP, sibling)
-    arrived(side_above, HIGH_DOWN)
+        send(SIDE_BELOW, part, up)
     for part in LAST_DOWN:
-        send(side_above, part, down)
-    send(side_above, HIGH_DOWN, sibling)
-    pass_on(side_below, LOW_DOWN)
-    pass_on(side_below, HIGH_DOWN)
-    pass_on(side_above, HIGH_UP)
-    pass_on(side_above, LOW_UP)
-    pass_on(far, HIGH_UP)
-    pass_on(far, HIGH_DOWN)
+        send(SIDE_ABOVE, part, down)
+    share(SIDE_BELOW, HIGH_UP, 2)
+    share(SIDE_ABOVE, HIGH_DOWN, 2)
+    lend(((FAR, LENT_ACROSS, across),), OWN_LENT + 1, (3, LOW_DOWN[1]))
+    lend(
+        ((SIDE_BELOW, LENT_UP, up), (SIDE_ABOVE, LENT_DOWN, down)),
+        OWN_LENT,
+        (2, HIGH_UP[1] + HIGH_DOWN[1]),
+    )
+    arrived(8)
+    for block, part in ARRIVALS[8]:
+        share(block, part)
     wait_bytes(norm_images.at[0, pl.ds(0, CHIPS - 1)], image_sem.at[1])
     remote(norm_images.at[core], both_sem.at[0], both_sem.at[1], rows=device(0, 0, 1)).start()
-    pass_on(side_far, LOW_UP)
-    for up_part, down_part in zip(LAST_UP[:2], LAST_DOWN[:2]):
-        pass_on(side_far, up_part)
-        pass_on(side_far, down_part)
-    pass_on(side_far, LAST_ACROSS[0])
-    pass_on(side_far, LAST_UP[2])
-    pass_on(side_far, LAST_DOWN[2])
-    pass_on(side_far, LAST_ACROSS[1])
-    assert len(places) == ARRIVALS
+    for line in range(9, OWN_LENT):
+        arrived(line)
+        for block, part in ARRIVALS[line]:
+            share(block, part)
+
+    @pl.when(core == 1)
+    def _():
+        for line in range(OWN_LENT, len(ARRIVALS)):
+            arrived(line)
+            for block, part in ARRIVALS[line]:
+                start(device(*block), part, 2, sibling_sem.at[1], device(0, 0, 1))
+            rows = sum(part[1] for _, part in ARRIVALS[line])
+            wait_rows(rows, recv_sem.at[line - OWN_LENT + SIBLING_LENT])
+            for block, part in ARRIVALS[line]:
+                start(device(*block, 1), part, 2, sibling_sem.at[1], device(0, 0, 1))
 
     wait_bytes(norm_images.at[0], both_sem.at[1])
     for j in range(CHIPS):
@@ -362,11 +414,22 @@
     wait_bytes(norm_images.at[0, pl.ds(0, CHIPS - 1)], image_sem.at[0])
     wait_bytes(norm_images.at[0], both_sem.at[0])
     wait_bytes(early, early_send.at[0])
-    wait_bytes(blocks.at[pl.ds(0, DEVICES // 2)], sibling_sem.at[0])
-    strips = rows_sent[0] // 8
-    count = next(n for n in range(1, DEVICES + 1) if strips % n == 0 and strips // n <= depth // 8)
-    wait_bytes(blocks.at[pl.ds(0, count), pl.ds(0, strips // count * 8), :], send_sem.at[0])
-    wait_bytes(blocks.at[pl.ds(0, DEVICES // 2)], send_sem.at[1])
+    wait_rows(2 * depth, sibling_sem.at[0])
+    lent = LENT_UP[1] + LENT_DOWN[1] + LENT_ACROSS[1]
+    other_rows = rows_sent[1] - 2 * depth - LOW_DOWN[1] - HIGH_UP[1] - HIGH_DOWN[1]
+
+    @pl.when(core == 0)
+    def _():
+        wait_rows(other_rows + 2 * lent, sibling_sem.at[1])
+
+    @pl.when(core == 1)
+    def _():
+        wait_rows(other_rows, sibling_sem.at[1])
+        wait_rows(rows_sent[2], send_sem.at[2])
+
+    assert rows_sent[2] == 4 * lent and rows_sent[1] + lent == DEVICES // 2 * depth
+    wait_rows(rows_sent[0], send_sem.at[0])
+    wait_rows(rows_sent[1], send_sem.at[1])
 
 
 def write_kernel(
@@ -455,9 +518,9 @@
             pltpu.VMEM((3, EARLY, wide), f32),
             dma((LOADS,)),
             dma((3,)),
-            dma((2,)),
-            dma((ARRIVALS,)),
-            dma((1,)),
+            dma((3,)),
+            dma((len(ARRIVALS) + 2,)),
+            dma((4,)),
             dma((2,)),
             dma((2,)),
             dma((1,)),

time: 70.1 us -> 69.9 us (level)
  no operation moved by 1% of the time
where the time goes in v6:
time: 69.9 us; the launch traced here: 69.8 us
  Pallas kernels  69.1 us (99%)
    pallas_call x1, Pallas kernels, shards(): pl.pallas_call(gather_kernel, out_shape=(pltpu.VMEM((DEVICES, depth, wide...  63.3 us
    pallas_call x1, Pallas kernels, shards(): pl.pallas_call(write_kernel, out_shape=(jax.ShapeDtypeStruct((DEVICES * d...  5.79 us

profile of v6, /device:TPU:1, one launch (start us, length us, event | category | flops | bytes accessed | tf_op | source)
XLA Modules:
  0.0 69.8 jit_solution(1342966436097023164)
XLA Ops:
  0.6 63.3 %gather.1 = (bf16[16,448,1152]{2,1,0:T(8,128)(2,1)S(1)}, f32[7,128]{1,0:T(8,128)S(1)}, f32[1,128]{1,0:T(1,128)S(1)}, f32[1,128]{1,0:T(1,128)S(1)}, bf16[56,128]{1,0:T(8,128)(2,1)S(1)}) custom-call(f32[448,896]{1,0:T(8,128)} %one_query.1, f32[448,896]{1,0:T(8,128)} %other_query.1, f32[448,128]{1,0:T(8,128)} %one_key.1, f32[448,128]{1,0:T(8,128)} %other_key.1, ...), custom_call_target="tpu_custom_call" | custom-call | tf_op jit(solution)/shard_map/gather/pallas_call | solution.py:494
  64.0 5.8 %write.1 = (bf16[7168,896]{1,0:T(8,128)(2,1)}, bf16[7168,128]{1,0:T(8,128)(2,1)}, bf16[7168,128]{1,0:T(8,128)(2,1)}, f32[7,128]{1,0:T(8,128)}, f32[1,128]{1,0:T(...) custom-call(bf16[16,448,1152]{2,1,0:T(8,128)(2,1)S(1)} %get-tuple-element.19.blocks, ...), custom_call_target="tpu_custom_call" | custom-call | tf_op jit(solution)/shard_map/write/pallas_call | solution.py:548

commit v7 on v6

--- a/solution.py
+++ b/solution.py
@@ -13,7 +13,7 @@
 NORM = 56
 
 LOW_UP, LOW_DOWN, HIGH_UP, HIGH_DOWN = (0, 104), (104, 96), (200, 120), (320, 128)
-EARLY = 40
+EARLY = 48
 LAST_UP = ((200, 40), (240, 48), (288, 16))
 LAST_DOWN = ((320, 64), (384, 32), (416, 16))
 LAST_ACROSS = ((104, 64), (168, 16))
@@ -142,10 +142,9 @@
     ):
         pltpu.make_async_copy(source, target, small_sem.at[i]).start()
     barrier = pltpu.get_barrier_semaphore()
-    for j in range(1, DEVICES):
-        pl.semaphore_signal(
-            barrier, inc=1, device_id={"rows": lax.rem(me + j, DEVICES)}, device_id_type=MESH
-        )
+    others = ((1, 2), (1, 1), (1, 3), (0, 2), (1, 0), (0, 1), (0, 3))
+    for goal in [device(dz, dy) for dz, dy in others] + [device(0, 0, 1)]:
+        pl.semaphore_signal(barrier, inc=1, device_id={"rows": goal}, device_id_type=MESH)
     for j in range(1, PEERS):
 
         @pl.when(place + j < PEERS)
@@ -188,9 +187,8 @@
     for t in range(tiles):
         sums[chip, :, pl.ds(t * LANES, LANES)] = jnp.sum(partial[t], axis=0, keepdims=True)
 
-    pl.semaphore_wait(barrier, DEVICES - 1 + place)
-
-    others = ((1, 2), (1, 1), (1, 3), (0, 2), (1, 0), (0, 1), (0, 3))
+    pl.semaphore_wait(barrier, CHIPS + place)
+
     for dz, dy in others:
         remote(sums.at[chip], sum_sem.at[0], sum_sem.at[1], rows=device(dz, dy)).start()
 

time: 69.9 us -> 69.5 us (level)
  no operation moved by 1% of the time
where the time goes in v7:
time: 69.5 us; the launch traced here: 69.4 us
  Pallas kernels  68.7 us (99%)
    pallas_call x1, Pallas kernels, shards(): pl.pallas_call(gather_kernel, out_shape=(pltpu.VMEM((DEVICES, depth, wide...  62.9 us
    pallas_call x1, Pallas kernels, shards(): pl.pallas_call(write_kernel, out_shape=(jax.ShapeDtypeStruct((DEVICES * d...  5.79 us

profile of v7, /device:TPU:1, one launch (start us, length us, event | category | flops | bytes accessed | tf_op | source)
XLA Modules:
  0.0 69.4 jit_solution(15538555875174714141)
XLA Ops:
  0.6 62.9 %gather.1 = (bf16[16,448,1152]{2,1,0:T(8,128)(2,1)S(1)}, f32[7,128]{1,0:T(8,128)S(1)}, f32[1,128]{1,0:T(1,128)S(1)}, f32[1,128]{1,0:T(1,128)S(1)}, bf16[56,128]{1,0:T(8,128)(2,1)S(1)}) custom-call(f32[448,896]{1,0:T(8,128)} %one_query.1, f32[448,896]{1,0:T(8,128)} %other_query.1, f32[448,128]{1,0:T(8,128)} %one_key.1, f32[448,128]{1,0:T(8,128)} %other_key.1, ...), custom_call_target="tpu_custom_call" | custom-call | tf_op jit(solution)/shard_map/gather/pallas_call | solution.py:492
  63.6 5.8 %write.1 = (bf16[7168,896]{1,0:T(8,128)(2,1)}, bf16[7168,128]{1,0:T(8,128)(2,1)}, bf16[7168,128]{1,0:T(8,128)(2,1)}, f32[7,128]{1,0:T(8,128)}, f32[1,128]{1,0:T(...) custom-call(bf16[16,448,1152]{2,1,0:T(8,128)(2,1)S(1)} %get-tuple-element.19.blocks, ...), custom_call_target="tpu_custom_call" | custom-call | tf_op jit(solution)/shard_map/write/pallas_call | solution.py:546

commit v8 on v7

--- a/solution.py
+++ b/solution.py
@@ -192,14 +192,14 @@
     for dz, dy in others:
         remote(sums.at[chip], sum_sem.at[0], sum_sem.at[1], rows=device(dz, dy)).start()
 
-    def row_copy(source, target):
-        return remote(norm_rows.at[source], row_send.at[0], row_recv.at[source], width=target)
+    def row_copy(source, target, rising):
+        return remote(norm_rows.at[source], row_send.at[0], row_recv.at[rising], width=target)
 
     for j in range(1, PEERS):
 
         @pl.when(place + j >= PEERS)
         def _():
-            row_copy(place, place + j - PEERS).start()
+            row_copy(place, place + j - PEERS, 0).start()
 
     up, down, across = (0, 1), (0, 3), (1, 0)
     early_parts = ((LOW_UP, up), (LOW_DOWN, down), (HIGH_UP, across))
@@ -208,7 +208,7 @@
             src_ref=mixed.at[pl.ds(part[0], EARLY), :],
             dst_ref=early.at[n],
             send_sem=early_send.at[0],
-            recv_sem=early_recv.at[n],
+            recv_sem=early_recv.at[0],
             device_id={"rows": device(*target)},
             device_id_type=MESH,
         ).start()
@@ -285,19 +285,24 @@
     send(own, HIGH_UP, down)
     for part in (LOW_UP, LOW_DOWN, HIGH_UP, HIGH_DOWN):
         share(own, part, 0)
+    wait_bytes(early, early_recv.at[0])
     for n, (block, (part, _)) in enumerate(zip((BELOW, ABOVE, SIDE), early_parts)):
-        wait_bytes(early.at[n], early_recv.at[n])
         narrow(early.at[n], 0, device(*block), part[0], EARLY)
 
     arrived(0)
     send(BELOW, LOW_UP, up)
     send(ABOVE, LOW_DOWN, down)
+    for p in range(PEERS - 1):
+
+        @pl.when(place == p)
+        def _():
+            wait_bytes(norm_rows.at[pl.ds(0, PEERS - 1 - p)], row_recv.at[0])
+
     for j in range(1, PEERS):
 
         @pl.when(place + j < PEERS)
         def _():
-            row_copy(place + j, place).wait_recv()
-            row_copy(place, place + j).start()
+            row_copy(place, place + j, 1).start()
 
     send(own, LOW_UP, across)
     send(own, LOW_DOWN, across)
@@ -320,11 +325,11 @@
     send(ABOVE, HIGH_DOWN, down)
     for block, part in ARRIVALS[4]:
         share(block, part)
-    for j in range(1, PEERS):
-
-        @pl.when(place + j >= PEERS)
-        def _():
-            row_copy(place + j - PEERS, place).wait_recv()
+    for p in range(1, PEERS):
+
+        @pl.when(place == p)
+        def _():
+            wait_bytes(norm_rows.at[pl.ds(0, p)], row_recv.at[1])
 
     flat = lax.broadcasted_iota(jnp.int32, (8, LANES), 0) * LANES + lax.broadcasted_iota(
         jnp.int32, (8, LANES), 1
@@ -522,11 +527,11 @@
             dma((2,)),
             dma((2,)),
             dma((1,)),
-            dma((PEERS,)),
+            dma((2,)),
             dma((2,)),
             dma((2,)),
             dma((1,)),
-            dma((3,)),
+            dma((1,)),
         ],
         compiler_params=pltpu.CompilerParams(
             collective_id=0, has_side_effects=True, vmem_limit_bytes=48 * 1024 * 1024

time: 69.5 us -> 69.4 us (level)
  no operation moved by 1% of the time
where the time goes in v8:
time: 69.4 us; the launch traced here: 69.3 us
  Pallas kernels  68.6 us (99%)
    pallas_call x1, Pallas kernels, shards(): pl.pallas_call(gather_kernel, out_shape=(pltpu.VMEM((DEVICES, depth, wide...  62.9 us
    pallas_call x1, Pallas kernels, shards(): pl.pallas_call(write_kernel, out_shape=(jax.ShapeDtypeStruct((DEVICES * d...  5.79 us

profile of v8, /device:TPU:1, one launch (start us, length us, event | category | flops | bytes accessed | tf_op | source)
XLA Modules:
  0.0 69.3 jit_solution(5047980807536314896)
XLA Ops:
  0.6 62.9 %gather.1 = (bf16[16,448,1152]{2,1,0:T(8,128)(2,1)S(1)}, f32[7,128]{1,0:T(8,128)S(1)}, f32[1,128]{1,0:T(1,128)S(1)}, f32[1,128]{1,0:T(1,128)S(1)}, bf16[56,128]{1,0:T(8,128)(2,1)S(1)}) custom-call(f32[448,896]{1,0:T(8,128)} %one_query.1, f32[448,896]{1,0:T(8,128)} %other_query.1, f32[448,128]{1,0:T(8,128)} %one_key.1, f32[448,128]{1,0:T(8,128)} %other_key.1, ...), custom_call_target="tpu_custom_call" | custom-call | tf_op jit(solution)/shard_map/gather/pallas_call | solution.py:497
  63.5 5.8 %write.1 = (bf16[7168,896]{1,0:T(8,128)(2,1)}, bf16[7168,128]{1,0:T(8,128)(2,1)}, bf16[7168,128]{1,0:T(8,128)(2,1)}, f32[7,128]{1,0:T(8,128)}, f32[1,128]{1,0:T(...) custom-call(bf16[16,448,1152]{2,1,0:T(8,128)(2,1)S(1)} %get-tuple-element.19.blocks, ...), custom_call_target="tpu_custom_call" | custom-call | tf_op jit(solution)/shard_map/write/pallas_call | solution.py:551

commit v9 on v7

--- a/solution.py
+++ b/solution.py
@@ -53,7 +53,7 @@
 )
 OWN_LENT = len(ARRIVALS) - 2
 SIBLING_LENT = len(ARRIVALS)
-LOADS = 4
+LOADS = 7
 
 
 def gather_kernel(
@@ -448,15 +448,17 @@
 ):
     depth = blocks.shape[1]
     outs = (query, key, value)
+    quarter = depth // 4
     for b in range(DEVICES):
-        at = 0
-        for n, out in enumerate(outs):
-            pltpu.make_async_copy(
-                blocks.at[b, :, pl.ds(at, out.shape[1])],
-                out.at[pl.ds(b * depth, depth), :],
-                sem.at[n],
-            ).start()
-            at += out.shape[1]
+        for i in range(4):
+            at = 0
+            for n, out in enumerate(outs):
+                pltpu.make_async_copy(
+                    blocks.at[b, pl.ds(i * quarter, quarter), pl.ds(at, out.shape[1])],
+                    out.at[pl.ds(b * depth + i * quarter, quarter), :],
+                    sem.at[n],
+                ).start()
+                at += out.shape[1]
     small = (
         (scale_query, query_scale),
         (scale_key, key_scale),

time: 69.5 us -> 69.4 us (level)
  no operation moved by 1% of the time
where the time goes in v9:
time: 69.4 us; the launch traced here: 69.3 us
  Pallas kernels  68.7 us (99%)
    pallas_call x1, Pallas kernels, shards(): pl.pallas_call(gather_kernel, out_shape=(pltpu.VMEM((DEVICES, depth, wide...  62.9 us
    pallas_call x1, Pallas kernels, shards(): pl.pallas_call(write_kernel, out_shape=(jax.ShapeDtypeStruct((DEVICES * d...  5.72 us

profile of v9, /device:TPU:1, one launch (start us, length us, event | category | flops | bytes accessed | tf_op | source)
XLA Modules:
  0.0 69.3 jit_solution(17907943603531570860)
XLA Ops:
  0.6 62.9 %gather.1 = (bf16[16,448,1152]{2,1,0:T(8,128)(2,1)S(1)}, f32[7,128]{1,0:T(8,128)S(1)}, f32[1,128]{1,0:T(1,128)S(1)}, f32[1,128]{1,0:T(1,128)S(1)}, bf16[56,128]{1,0:T(8,128)(2,1)S(1)}) custom-call(f32[448,896]{1,0:T(8,128)} %one_query.1, f32[448,896]{1,0:T(8,128)} %other_query.1, f32[448,128]{1,0:T(8,128)} %one_key.1, f32[448,128]{1,0:T(8,128)} %other_key.1, ...), custom_call_target="tpu_custom_call" | custom-call | tf_op jit(solution)/shard_map/gather/pallas_call | solution.py:494
  63.6 5.7 %write.1 = (bf16[7168,896]{1,0:T(8,128)(2,1)}, bf16[7168,128]{1,0:T(8,128)(2,1)}, bf16[7168,128]{1,0:T(8,128)(2,1)}, f32[7,128]{1,0:T(8,128)}, f32[1,128]{1,0:T(...) custom-call(bf16[16,448,1152]{2,1,0:T(8,128)(2,1)S(1)} %get-tuple-element.19.blocks, ...), custom_call_target="tpu_custom_call" | custom-call | tf_op jit(solution)/shard_map/write/pallas_call | solution.py:548
